TPU v7x, 256 devices: a whole 4x4x8 slice. The times are simulated.
256 devices in a mesh: stn: 4 (over z_hi), chan: 64 (over x, z_lo, y, core).
Axes of the slice: x: 4, y: 4, z: 8 (z_hi: 4, z_lo: 2; z = z_hi * 2 + z_lo), core: 2. Of those that a mesh axis runs over, the one named last changes fastest.
Arguments:
- voltages: bfloat16 [1024, 64, 8, 1024], P('stn', 'chan'), may hold values from -6 to 6
- fir_taps: float32 [8, 8, 1024], replicated, may hold values from -2.5 to 2.5
Outputs:
- visibilities: float32 [4, 64, 2, 1024, 1024], P(None, 'chan', None, 'stn')
All inputs are finite; a program needn't handle non-finite values.
Results may differ from a plain program's by a relative error of at most 0.0044.
Values may be sent and summed in bfloat16 or wider, within the bound.
A program may use at most 128 MiB of HBM per device.

v0:
```python
import math

import jax
import jax.numpy as jnp
from jax import lax
from jax.sharding import PartitionSpec as P

AVG = 16


def shifted(block, axis, distance):
    devices = range(lax.axis_size(axis))
    route = [(i - distance, i) for i in devices if i - distance in devices]
    return lax.ppermute(block, axis, route)


def rotation(numbers, modulus):
    angles = (numbers % modulus).astype(jnp.float32) * jnp.float32(-2.0 * math.pi / modulus)
    return (jnp.cos(angles), jnp.sin(angles))


def split_pair(table):
    upper = table.astype(jnp.bfloat16)
    lower = (table - upper.astype(jnp.float32)).astype(jnp.bfloat16)
    return (upper, lower)


def complex_table(real_part, imag_part, axis_at):
    first = jnp.stack([real_part, imag_part], axis=-1)
    second = jnp.stack([-imag_part, real_part], axis=-1)
    return jnp.stack([first, second], axis=axis_at)


def per_device(voltages, fir_taps):
    inputs_dev, _, frames_dev, slot_count = voltages.shape
    phases = fir_taps.shape[0]
    tap_count = fir_taps.shape[1]
    lane_count = lax.axis_size("chan")
    groups = lane_count // phases
    position = lax.axis_index("chan")
    my_phase = position % phases
    my_group = position // phases
    recent = voltages[:, 0]
    earlier = shifted(voltages[:, 0, frames_dev - (tap_count - 1) :, :], "chan", phases)
    series = jnp.concatenate([earlier, recent], axis=1)
    coeffs = lax.dynamic_index_in_dim(fir_taps, my_phase, 0, keepdims=False)
    frame_ids = my_group * frames_dev + jnp.arange(frames_dev, dtype=jnp.int32)
    keep_mask = (frame_ids >= tap_count - 1).astype(jnp.float32)
    filtered = sum(
        (
            coeffs[tap_index]
            * series[:, tap_count - 1 - tap_index : tap_count - 1 - tap_index + frames_dev].astype(
                jnp.float32
            )
            for tap_index in range(tap_count)
        )
    )
    filtered = filtered * keep_mask[None, :, None]
    better = lax.Precision.HIGH
    split_len = slot_count // phases
    folded = filtered.reshape(inputs_dev, frames_dev, split_len, phases)
    slot_ids = jnp.arange(split_len, dtype=jnp.int32)
    short_re, short_im = rotation(slot_ids[:, None] * slot_ids[None, :], split_len)
    short_table = jnp.stack([short_re, short_im], axis=-1)
    inner = jnp.einsum(
        "ifqr,qvc->rvcfi", folded, short_table, precision=better, preferred_element_type=jnp.float32
    )
    rest_ids = jnp.arange(phases, dtype=jnp.int32)
    freq_ids = jnp.arange(slot_count, dtype=jnp.int32).reshape(phases, split_len)
    twist_re, twist_im = rotation(
        (my_phase + phases * rest_ids)[:, None, None] * freq_ids[None], phases * slot_count
    )
    twist_table = complex_table(twist_re, twist_im, 3)
    branch = jnp.einsum(
        "rvcfi,ruvcd->uvfdi",
        inner,
        twist_table,
        precision=better,
        preferred_element_type=jnp.float32,
    )
    branch = branch.reshape(slot_count, 1, frames_dev, 2, inputs_dev).astype(jnp.bfloat16)
    band_count = phases // 2
    band_re, band_im = rotation(
        rest_ids[:, None] * jnp.arange(band_count, dtype=jnp.int32)[None, :], phases
    )
    band_table = complex_table(band_re, band_im, 1)
    band_upper, band_lower = split_pair(band_table)
    turned = lax.all_to_all(branch, "chan", split_axis=0, concat_axis=1, tiled=True)
    span_len = turned.shape[0]
    sources = turned.shape[1]
    item_count = turned.shape[2]
    grouped = turned.reshape(span_len, sources // phases, phases, item_count, 2, inputs_dev)
    phase_form = "wgpfci,pcbd->bwgfdi"
    total = jnp.einsum(
        phase_form, grouped, band_upper, preferred_element_type=jnp.float32
    ) + jnp.einsum(phase_form, grouped, band_lower, preferred_element_type=jnp.float32)
    spectra = total.astype(jnp.bfloat16)
    span_dev = spectra.shape[1]
    subs_dev = span_dev // AVG
    stacked = spectra.reshape(band_count, subs_dev, AVG * groups * frames_dev, 2, inputs_dev)
    columns = stacked.reshape(band_count, subs_dev, -1, inputs_dev)
    swapped = jnp.stack([stacked[:, :, :, 1], -stacked[:, :, :, 0]], axis=3).reshape(
        band_count, subs_dev, -1, inputs_dev
    )
    left_side = jnp.stack([columns, swapped], axis=2)
    spectra_count = groups * frames_dev - (tap_count - 1)
    scaling = 1.0 / (phases * slot_count * AVG * spectra_count)
    vis_form = "bsokn,bskw->bsonw"
    return (
        jnp.einsum(
            vis_form,
            left_side,
            lax.all_gather(columns, "stn", axis=3, tiled=True),
            preferred_element_type=jnp.float32,
        )
        * scaling
    )


def solution(mesh):
    return jax.shard_map(
        per_device,
        mesh=mesh,
        in_specs=(P("stn", "chan", None, None), P()),
        out_specs=P(None, "chan", None, "stn", None),
        check_vma=False,
    )
```

profile of v0, /device:TPU:3, one launch (start us, length us, event | category | flops | bytes accessed | tf_op | source)
XLA Modules:
  0.0 652.6 jit_solution(3090252074284352007)
XLA Ops:
  6.5 6.9 %copy.51 = bf16[256,1,8,1024]{0,3,2,1:T(8,128)(2,1)} copy(bf16[256,1,8,1024]{3,2,1,0:T(8,128)(2,1)} %param.2) | data formatting | bytes 8388608 | tf_op args[0]
  13.4 4.1 slice_bitcast_fusion
  17.5 3.5 collective-permute-start
  21.1 0.2 fusion.47
  21.3 0.5 copy.49
  21.9 0.5 copy.50
  22.4 1.1 constant_dynamic-slice_fusion.6
  23.5 0.3 fusion.45
  23.8 77.0 %collective-permute-done = bf16[256,7,1024]{0,2,1:T(8,128)(2,1)} collective-permute-done((bf16[256,7,1024]{0,2,1:T(8,128)(2,1)}, bf16[256,7,1024]{0,2,1:T(8,128)(2,1)}, u32[]{:S(2)}, u32[]{:S(2)}) %collective-permute-start) | collective-permute-done | bytes 3670048 | tf_op jit(solution)/shard_map/ppermute | solution.py:14
  100.8 17.1 %multiply_bitcast_fusion.1 = f32[256,8,128,8]{0,3,2,1:T(8,128)} fusion(bf16[256,8,1024]{0,2,1:T(8,128)(2,1)} %bitcast.117, bf16[256,7,1024]{0,2,1:T(8,128)(2,1)} %collective-permute-done, f32[8]{0:T(128)S(1)} %compare_convert_fusion, f32[1024]{0:T(1024)S(1)} %bitcast.129, f32[1024]{0:T(1024)S(1)} %bitcast.123, f32[1024]{0:T(1024)S(1)} %bitcast.124, ...), kind=kLoop, calls=%fused_computation.30 | loop fusion | flops 65011712 | bytes 16285728 | tf_op jit(solution)/shard_map/reshape | solution.py:61
  118.0 9.1 %copy.54 = f32[256,8,128,8]{2,0,3,1:T(8,128)} copy(f32[256,8,128,8]{0,3,2,1:T(8,128)} %multiply_bitcast_fusion.1) | data formatting | bytes 16777216 | tf_op jit(solution)/shard_map/reshape | solution.py:61
  127.1 14.1 %fusion.18 = f32[8,128,2,8,256,1]{4,1,0,3,2,5:T(8,128)} fusion(f32[256,8,128,8]{2,0,3,1:T(8,128)} %copy.54, f32[128,128,1]{1,0,2:T(8,128)S(1)} %get-tuple-element.22, f32[128,128,1]{1,0,2:T(8,128)S(1)} %get-tuple-element.23), kind=kOutput, calls=%fused_computation.33 | convolution fusion | flops 3221258240 | bytes 25296896 | tf_op jit(solution)/shard_map/ifqr,qvc->rvcfi/dot_general | solution.py:65
  141.2 24.8 %fusion.4 = bf16[8,128,8,2,256]{4,0,2,3,1:T(8,128)(2,1)} fusion(f32[8,128,2,8,256,1]{4,1,0,3,2,5:T(8,128)} %fusion.18, f32[8,8,128,1,2]{0,1,3,4,2:T(8,128)S(1)} %bitcast.121, f32[8,8,128,1,2]{0,1,3,4,2:T(8,128)S(1)} %bitcast.120), kind=kOutput, calls=%fused_computation.17 | convolution fusion | flops 406880256 | bytes 25296896 | tf_op jit(solution)/shard_map/rvcfi,ruvcd->uvfdi/dot_general | solution.py:74
  166.0 8.4 %copy.56 = bf16[8,128,8,2,256]{4,2,3,1,0:T(8,128)(2,1)} copy(bf16[8,128,8,2,256]{4,0,2,3,1:T(8,128)(2,1)} %fusion.4) | data formatting | bytes 16777216 | tf_op jit(solution)/shard_map/convert_element_type | solution.py:81
  174.4 10.0 %all-to-all-start = ((bf16[1024,1,8,2,256]{4,2,3,1,0:T(8,128)(2,1)}), bf16[1024,1,8,2,256]{4,2,3,1,0:T(8,128)(2,1)}, u32[]{:S(2)}, u32[]{:S(2)}) async-start(bf16[1024,1,8,2,256]{4,2,3,1,0:T(8,128)(2,1)} %bitcast.118), calls=%async_computation | async-start | bytes 16777216 | tf_op jit(solution)/shard_map/all_to_all | solution.py:88
  184.4 0.0 all-gather.2.cloned.1.call-start
  184.4 0.1 fusion.61
  184.5 0.1 fusion.59
  184.6 105.0 %all-to-all-done = bf16[1024,1,8,2,256]{4,2,3,1,0:T(8,128)(2,1)} async-done(((bf16[1024,1,8,2,256]{4,2,3,1,0:T(8,128)(2,1)}), bf16[1024,1,8,2,256]{4,2,3,1,0:T(8,128)(2,1)}, u32[]{:S(2)}, u32[]{:S(2)}) %all-to-all-start) | async-done | bytes 8388640 | tf_op jit(solution)/shard_map/all_to_all | solution.py:88
  289.6 12.6 %fusion.8 = f32[4,2,16,8,8,256,1]{5,0,6,4,3,2,1:T(4,128)} fusion(bf16[16,8,8,8,2,256]{5,3,4,0,2,1:T(8,128)(2,1)} %bitcast.32, f32[8,1,4,2]{0,2,1,3:T(4,128)S(1)} %get-tuple-element.19, f32[8,1,4,2]{0,2,1,3:T(4,128)S(1)} %get-tuple-element.18), kind=kOutput, calls=%fused_computation.23 | convolution fusion | flops 67109504 | bytes 16777728 | tf_op jit(solution)/shard_map/wgpfci,pcbd->bwgfdi/dot_general | solution.py:96
  302.2 16.9 %fusion.7 = bf16[4,2,16,8,8,256]{5,0,4,3,2,1:T(4,128)(2,1)} fusion(f32[4,2,16,8,8,256,1]{5,0,6,4,3,2,1:T(4,128)} %fusion.8, bf16[16,8,8,8,2,256]{5,3,4,0,2,1:T(8,128)(2,1)} %bitcast.32, f32[8,1,4,2]{0,2,1,3:T(4,128)S(1)} %get-tuple-element.19, f32[8,1,4,2]{0,2,1,3:T(4,128)S(1)} %get-tuple-element.18), kind=kOutput, calls=%fused_computation.22 | convolution fusion | flops 71303680 | bytes 20972032 | tf_op jit(solution)/shard_map/wgpfci,pcbd->bwgfdi/dot_general | solution.py:94
  319.1 4.3 copy.60
  323.4 1.9 copy-done
  325.4 2.6 copy.66
  327.9 0.0 all-gather.2.cloned.1.call-update
  327.9 2.3 slice_bitcast_fusion.2
  330.3 2.4 fusion.31
  332.7 4.7 pad_maximum_fusion.1
  337.4 7.6 %copy.64 = bf16[4,1,1,2048,256]{3,4,2,0,1:T(8,128)(2,1)} copy(bf16[4,1,1,2048,256]{4,0,3,2,1:T(4,128)(2,1)} %bitcast.119) | data formatting | bytes 8388608 | tf_op jit(solution)/shard_map/stack;reshape | solution.py:105
  345.0 7.9 %copy.63 = bf16[4,1,1,2048,256]{3,4,2,0,1:T(8,128)(2,1)} copy(bf16[4,1,1,2048,256]{4,0,3,2,1:T(4,128)(2,1)} %bitcast.116) | data formatting | bytes 8388608 | tf_op jit(solution)/shard_map/stack;reshape;reshape | solution.py:105
  352.9 275.6 %all-gather.2.cloned.1.call-done = bf16[4,1,2048,1024]{3,2,0,1:T(8,128)(2,1)} async-done(((bf16[4,1,2048,256]{3,2,0,1:T(8,128)(2,1)}), bf16[4,1,2048,1024]{3,2,0,1:T(8,128)(2,1)}) %all-gather.2.cloned.1.call-update) | async-done | bytes 16777232 | tf_op jit(solution)/shard_map/all_gather | solution.py:113
  628.4 16.9 %multiply_bitcast_fusion = f32[4,1,2,256,1024]{4,3,2,1,0:T(8,128)} fusion(bf16[4,1,2048,1024]{3,2,0,1:T(8,128)(2,1)} %all-gather.2.cloned.1.call-done, bf16[4,1,1,2048,256]{3,4,2,0,1:T(8,128)(2,1)} %copy.64, bf16[4,1,1,2048,256]{3,4,2,0,1:T(8,128)(2,1)} %copy.63), kind=kOutput, calls=%fused_computation.29 | convolution fusion | flops 8596226048 | bytes 33554432 | tf_op jit(solution)/shard_map/bsokn,bskw->bsonw/dot_general | solution.py:110
  (6 shorter events, 0.0 us)
Async XLA Ops:
  17.5 83.3 %collective-permute-start = (bf16[256,7,1024]{0,2,1:T(8,128)(2,1)}, bf16[256,7,1024]{0,2,1:T(8,128)(2,1)}, u32[]{:S(2)}, u32[]{:S(2)}) collective-permute-start(bf16[256,7,1024]{0,2,1:T(8,128)(2,1)} %slice_bitcast_fusion), channel_id=1, source_target_pairs={{0,8},{1,9},{2,10},{3,11},{4,12},{5,13},{6,14},{7,15},{8,16},{9,17... | collective-permute-start | bytes 11010056 | tf_op jit(solution)/shard_map/ppermute | solution.py:14
  174.4 115.2 %all-to-all-start = ((bf16[1024,1,8,2,256]{4,2,3,1,0:T(8,128)(2,1)}), bf16[1024,1,8,2,256]{4,2,3,1,0:T(8,128)(2,1)}, u32[]{:S(2)}, u32[]{:S(2)}) async-start(bf16[1024,1,8,2,256]{4,2,3,1,0:T(8,128)(2,1)} %bitcast.118), calls=%async_computation | async-start | bytes 16777216 | tf_op jit(solution)/shard_map/all_to_all | solution.py:88
  184.4 444.0 %all-gather.2.cloned.1.call-start = ((), (), s32[]{:S(2)}) async-start(), calls=%async_computation.1 | async-start | bytes 20971520 | tf_op jit(solution)/shard_map/all_gather | solution.py:113
  323.4 1.9 copy-start
Sparse Core Ops, SparseCore 0:
  328.1 300.3 all-gather.1
where the time goes:
time: 661 us; the launch traced here: 653 us
  waiting for transfers between devices  458 us (69%)
  matrix products  85.3 us (13%)
  local copies, waits for them, and re-layouts  57.2 us (9%)
  other arithmetic  24.9 us (4%)
  between operations  14 us (2%)
  starting transfers between devices  13.6 us (2%)
    all_gather x1, waiting for transfers between devices, per_device(): lax.all_gather(columns, 'stn', axis=3, tiled=True)  276 us
    all_to_all x1, waiting for transfers between devices, per_device(): lax.all_to_all(branch, 'chan', split_axis=0, concat_axis=1, tiled=True)  105 us
    ppermute x1, waiting for transfers between devices, shifted(): return lax.ppermute(block, axis, route)  77 us
    dot_general x1, matrix products, per_device(): jnp.einsum('rvcfi,ruvcd->uvfdi', inner, twist_table, precision=better, pr...  24.8 us
    reshape x1, other arithmetic, per_device(): folded = filtered.reshape(inputs_dev, frames_dev, split_len, phases)  17.1 us
    dot_general x1, matrix products, per_device(): jnp.einsum(phase_form, grouped, band_upper, preferred_element_type=jnp.fl...  16.9 us
    dot_general x1, matrix products, per_device(): jnp.einsum(vis_form, left_side, lax.all_gather(columns, 'stn', axis=3, ti...  16.9 us
    another operation x2, local copies, waits for them, and re-layouts, per_device(): left_side = jnp.stack([columns, swapped], axis=2)  15.5 us
  transfers between devices with their start and end apart: 3, of which 3 were waited for; matrix products, arithmetic and copies ran while one was open for 4% of the time, Pallas kernels for 0%

commit v1 on v0

v1 whole, which is shorter than its diff:
```python
import math

import jax
import jax.numpy as jnp
import numpy as np
from jax import lax
from jax.experimental import pallas as pl
from jax.experimental.pallas import tpu as pltpu
from jax.sharding import PartitionSpec as P

AVG = 16
LANES = 128


def dft_table(slots):
    half = slots // 2
    q = np.arange(slots, dtype=np.int64).reshape(half, 2).T
    turns = (q[:, :, None] * np.arange(half, dtype=np.int64)) % slots
    angles = turns.astype(np.float64) * (-2.0 * math.pi / slots)
    table = np.concatenate([np.cos(angles), np.sin(angles)], axis=1).astype(np.float32)
    upper = table.astype(jnp.bfloat16)
    lower = (table - upper.astype(np.float32)).astype(jnp.bfloat16)
    return np.concatenate([upper, lower], axis=2)


def first_twist(slots, phases):
    half = slots // 2
    q = jnp.arange(slots, dtype=jnp.int32).reshape(half, 2).T
    q = jnp.broadcast_to(q[:, :, None], (2, half, LANES))
    angles = q.astype(jnp.float32) * jnp.float32(-2.0 * math.pi / (phases * slots))
    return jnp.stack([jnp.cos(angles), jnp.sin(angles)])


def channelise_kernel(spectra_count, a_ref, fir_ref, tab_ref, t1_ref, o_ref, xs, g, br, tw):
    phase = pl.program_id(0)
    groups, _, inputs, fr, slots = a_ref.shape
    frames = groups * fr
    taps = fir_ref.shape[1]
    half = slots // 2
    rows = inputs * frames

    @pl.when(phase == 0)
    def _():
        tw[0] = jnp.ones(tw.shape[1:], jnp.float32)
        tw[1] = jnp.zeros(tw.shape[1:], jnp.float32)
        xs[:, frames:, :] = jnp.zeros((inputs, xs.shape[1] - frames, slots), jnp.float32)

    for i in range(inputs):
        for grp in range(groups):
            xs[i, grp * fr : (grp + 1) * fr, :] = a_ref[grp, 0, i].astype(jnp.float32)

    keep = lax.broadcasted_iota(jnp.int32, (frames, LANES), 0) < spectra_count

    @pl.loop(0, inputs)
    def _(i):
        for chunk in range(half // LANES):

            def fir(at):
                total = None
                for k in range(taps):
                    term = fir_ref[0, k : k + 1, at : at + LANES] * xs[
                        i, taps - 1 - k : taps - 1 - k + frames, at : at + LANES
                    ]
                    total = term if total is None else total + term
                return jnp.where(keep, total, 0.0)

            at = chunk * LANES
            low, high = fir(at), fir(at + half)
            row = pl.multiple_of(i * frames, frames)
            for par, value in ((0, low + high), (1, low - high)):
                upper = value.astype(jnp.bfloat16)
                lower = (value - upper.astype(jnp.float32)).astype(jnp.bfloat16)
                g[par, pl.ds(row, frames), at : at + LANES] = upper
                g[par, pl.ds(row, frames), half + at : half + at + LANES] = upper
                g[par, pl.ds(row, frames), 2 * half + at : 2 * half + at + LANES] = lower

    step = 256
    dims = (((1,), (1,)), ((), ()))

    for par in range(2):

        @pl.loop(0, half // step)
        def _(block):
            def product(start):
                at = pl.multiple_of(start + block * step, step)
                first = tab_ref[par, pl.ds(at, step), :]
                return lax.dot_general(
                    first, g[par, :, : 2 * half], dims, preferred_element_type=jnp.float32
                ) + lax.dot_general(
                    first[:, :half], g[par, :, 2 * half :], dims, preferred_element_type=jnp.float32
                )

            real, imag = product(0), product(half)
            at = pl.multiple_of(block * step, step)
            cos = tw[0, par, pl.ds(at, step), :]
            sin = tw[1, par, pl.ds(at, step), :]
            for part in range(rows // LANES):
                re = real[:, part * LANES : (part + 1) * LANES]
                im = imag[:, part * LANES : (part + 1) * LANES]
                br[phase, 0, par, part, pl.ds(at, step), :] = (re * cos - im * sin).astype(jnp.bfloat16)
                br[phase, 1, par, part, pl.ds(at, step), :] = (re * sin + im * cos).astype(jnp.bfloat16)

    cos, sin = tw[0], tw[1]
    tw[0] = cos * t1_ref[0] - sin * t1_ref[1]
    tw[1] = cos * t1_ref[1] + sin * t1_ref[0]

    @pl.when(phase == pl.num_programs(0) - 1)
    def _():
        root = math.sqrt(0.5)
        tile = 16
        left = lax.broadcasted_iota(jnp.int32, (tile, LANES), 1) < frames

        def four(a, b, c, d):
            (ar, ai), (b_r, bi), (cr, ci), (dr, di) = a, b, c, d
            er, ei, fr_, fi = ar + cr, ai + ci, ar - cr, ai - ci
            gr, gi, hr, hi = b_r + dr, bi + di, b_r - dr, bi - di
            return ((er + gr, ei + gi), (fr_ + hi, fi - hr), (er - gr, ei - gi), (fr_ - hi, fi + hr))

        @pl.loop(0, half // tile)
        def _(block):
            at = pl.multiple_of(block * tile, tile)
            for part in range(rows // LANES):
                lines = []
                for par in range(2):
                    b = [
                        tuple(br[p, ri, par, part, pl.ds(at, tile), :].astype(jnp.float32) for ri in range(2))
                        for p in range(8)
                    ]
                    even = four(b[0], b[2], b[4], b[6])
                    odd = four(b[1], b[3], b[5], b[7])
                    (o1r, o1i), (o2r, o2i), (o3r, o3i) = odd[1:]
                    turned = (
                        odd[0],
                        ((o1r + o1i) * root, (o1i - o1r) * root),
                        (o2i, -o2r),
                        ((o3i - o3r) * root, (-o3r - o3i) * root),
                    )
                    lines.append([(e[0] + o[0], e[1] + o[1]) for e, o in zip(even, turned)])
                for c in range(4):
                    firsts, seconds = [], []
                    for par in range(2):
                        re, im = lines[par][c]
                        firsts.append(jnp.where(left, re, pltpu.roll(im, frames, 1)).reshape(2, 8, LANES))
                        seconds.append(jnp.where(left, pltpu.roll(re, frames, 1), im).reshape(2, 8, LANES))
                    for i, pair in ((2 * part, firsts), (2 * part + 1, seconds)):
                        both = jnp.concatenate(pair, axis=1)
                        o_ref[c, pl.ds(block * 2, 2), i] = both.astype(jnp.bfloat16)


def channelise(samples, fir_taps, spectra_count):
    groups, phases, inputs, fr, slots = samples.shape
    frames = groups * fr
    taps = fir_taps.shape[1]
    half = slots // 2
    rows = inputs * frames
    table = jnp.asarray(dft_table(slots))
    twist = first_twist(slots, phases)
    whole = pl.BlockSpec(memory_space=pltpu.VMEM)
    return pl.pallas_call(
        lambda *refs: channelise_kernel(spectra_count, *refs),
        grid=(phases,),
        out_shape=jax.ShapeDtypeStruct((4, slots // AVG, inputs, AVG, 2 * frames), jnp.bfloat16),
        in_specs=[
            pl.BlockSpec((groups, 1, inputs, fr, slots), lambda p: (0, p, 0, 0, 0)),
            pl.BlockSpec((1, taps, slots), lambda p: (p, 0, 0)),
            whole,
            whole,
        ],
        out_specs=whole,
        scratch_shapes=[
            pltpu.VMEM((inputs, frames + 8, slots), jnp.float32),
            pltpu.VMEM((2, rows, 3 * half), jnp.bfloat16),
            pltpu.VMEM((phases, 2, 2, rows // LANES, half, LANES), jnp.bfloat16),
            pltpu.VMEM((2, 2, half, LANES), jnp.float32),
        ],
        compiler_params=pltpu.CompilerParams(vmem_limit_bytes=60 << 20),
        cost_estimate=pl.CostEstimate(flops=20 * 10**9, bytes_accessed=20 << 20, transcendentals=0),
    )(samples, fir_taps, table, twist)


def correlate_kernel(scaling, r_ref, o_ref, wide, x, y):
    inputs, items, lanes = r_ref.shape
    step = 256
    dims = (((1,), (1,)), ((), ()))
    sub = 128

    @pl.loop(0, inputs // sub)
    def _(block):
        row = pl.multiple_of(block * sub, sub)
        wide[...] = r_ref[pl.ds(row, sub)].astype(jnp.float32).reshape(sub * items, lanes)
        left = lax.broadcasted_iota(jnp.int32, (sub, lanes), 1) < lanes // 2
        for item in range(items):
            value = wide[pl.ds(item, sub, stride=items), :]
            turned = pltpu.roll(value, lanes // 2, 1)
            at = item * lanes
            x[pl.ds(row, sub), at : at + lanes] = value.astype(jnp.bfloat16)
            y[pl.ds(row, sub), at : at + lanes] = jnp.where(left, turned, -turned).astype(jnp.bfloat16)

    @pl.loop(0, inputs // step)
    def _(block):
        row = pl.multiple_of(block * step, step)
        for part, source in ((0, x), (1, y)):
            for col in range(0, inputs, step):
                product = lax.dot_general(
                    source[pl.ds(row, step), :], x[col : col + step, :], dims, preferred_element_type=jnp.float32
                )
                o_ref[block, part, :, col : col + step] = (product * scaling).astype(jnp.bfloat16)


def correlate(gathered, scaling):
    inputs, items, lanes = gathered.shape
    whole = pl.BlockSpec(memory_space=pltpu.VMEM)
    return pl.pallas_call(
        lambda *refs: correlate_kernel(scaling, *refs),
        out_shape=jax.ShapeDtypeStruct((inputs // 256, 2, 256, inputs), jnp.bfloat16),
        in_specs=[whole],
        out_specs=whole,
        scratch_shapes=[
            pltpu.VMEM((128 * items, lanes), jnp.float32),
            pltpu.VMEM((inputs, items * lanes), jnp.bfloat16),
            pltpu.VMEM((inputs, items * lanes), jnp.bfloat16),
        ],
        compiler_params=pltpu.CompilerParams(vmem_limit_bytes=60 << 20),
        cost_estimate=pl.CostEstimate(flops=9 * 10**9, bytes_accessed=8 << 20, transcendentals=0),
    )(gathered)


def per_device(voltages, fir_taps):
    inputs_dev, _, fr, slots = voltages.shape
    phases, taps, _ = fir_taps.shape
    lane_count = lax.axis_size("chan")
    stations = lax.axis_size("stn")
    groups = lane_count // phases
    own = inputs_dev // lane_count
    frames = groups * fr
    spectra_count = frames - (taps - 1)
    dealt = lax.all_to_all(voltages[:, 0], "chan", 0, 0, tiled=True)
    samples = dealt.reshape(groups, phases, own, fr, slots)
    spectra = channelise(samples, fir_taps, spectra_count)
    spectra = spectra.reshape(stations * lane_count * own, AVG, 2 * frames)
    gathered = lax.all_to_all(spectra, ("stn", "chan"), 0, 0, tiled=True)
    scaling = 1.0 / (phases * slots * AVG * spectra_count)
    rows = correlate(gathered, scaling)
    mine = lax.all_to_all(rows, "stn", 0, 0, tiled=True)
    return mine.astype(jnp.float32)[:, None]


def solution(mesh):
    return jax.shard_map(
        per_device,
        mesh=mesh,
        in_specs=(P("stn", "chan", None, None), P()),
        out_specs=P(None, "chan", None, "stn", None),
        check_vma=False,
    )
```

time: 661 us -> 337 us (0.51)
  the two profiles are of different devices: /device:TPU:3 before, /device:TPU:24 now
where the time goes in v1:
time: 337 us
  blocking collectives  212 us (63%)
  Pallas kernels  61.9 us (18%)
  waiting for transfers between devices  48.2 us (14%)
  starting transfers between devices  9.25 us (3%)
  other arithmetic  5.63 us (2%)
    all_to_all x1, blocking collectives, per_device(): gathered = lax.all_to_all(spectra, ('stn', 'chan'), 0, 0, tiled=True)  112 us
    all_to_all x1, blocking collectives, per_device(): mine = lax.all_to_all(rows, 'stn', 0, 0, tiled=True)  99.5 us
    all_to_all x1, waiting for transfers between devices, per_device(): dealt = lax.all_to_all(voltages[:, 0], 'chan', 0, 0, tiled=True)  48.2 us
    pallas_call x1, Pallas kernels, channelise(): pl.pallas_call(lambda *refs: channelise_kernel(spectra_count, *refs), gri...  43.8 us
    pallas_call x1, Pallas kernels, correlate(): pl.pallas_call(lambda *refs: correlate_kernel(scaling, *refs), out_shape=...  18.1 us
    all_to_all x1, starting transfers between devices, per_device(): dealt = lax.all_to_all(voltages[:, 0], 'chan', 0, 0, tiled=True)  9.25 us
  transfers between devices with their start and end apart: 1, of which 1 were waited for; matrix products, arithmetic and copies ran while one was open for 0% of the time, Pallas kernels for 0%

profile of v1, /device:TPU:24, one launch (start us, length us, event | category | flops | bytes accessed | tf_op | source)
XLA Modules:
  0.0 336.9 jit_solution(13801304481689989039)
XLA Ops:
  0.0 9.3 %all-to-all-start = ((bf16[256,8,1024]{2,1,0:T(8,128)(2,1)}), bf16[256,8,1024]{2,1,0:T(8,128)(2,1)}, u32[]{:S(2)}, u32[]{:S(2)}) async-start(bf16[256,8,1024]{2,1,0:T(8,128)(2,1)} %bitcast.9), calls=%async_computation | async-start | bytes 8388608 | tf_op jit(solution)/shard_map/all_to_all | solution.py:237
  9.3 0.1 fusion.1
  9.3 0.1 fusion
  9.4 0.2 broadcast_in_dim.15
  9.6 0.2 broadcast_in_dim.14
  9.8 1.0 pad_maximum_fusion.refs_3_
  10.9 48.2 %all-to-all-done = bf16[256,8,1024]{2,1,0:T(8,128)(2,1)} async-done(((bf16[256,8,1024]{2,1,0:T(8,128)(2,1)}), bf16[256,8,1024]{2,1,0:T(8,128)(2,1)}, u32[]{:S(2)}, u32[]{:S(2)}) %all-to-all-start) | async-done | bytes 4194336 | tf_op jit(solution)/shard_map/all_to_all | solution.py:237
  59.0 43.8 %shard_map.37 = bf16[4,64,4,16,128]{4,3,2,1,0:T(8,128)(2,1)} custom-call(bf16[8,8,4,8,1024]{4,3,2,1,0:T(8,128)(2,1)} %bitcast.1.refs_0_, f32[8,8,1024]{2,1,0:T(8,128)} %refs_1_.1, bf16[2,1024,1024]{2,1,0:T(8,128)(2,1)} %constant.6.clone.refs_2_, f32[2,2,512,128]{3,2,1,0:T(8,128)} %pad_maximum_fusion.refs_3_), custom_call_target="tpu_custom_call" | custom-call | flops 20000000000 | bytes 20971520 | tf_op jit(solution)/shard_map/pallas_call | solution.py:159
  102.9 112.1 %all_to_all.15.refs_0_ = bf16[1024,16,128]{2,1,0:T(8,128)(2,1)} all-to-all(bf16[1024,16,128]{2,1,0:T(8,128)(2,1)} %bitcast.10), channel_id=1, replica_groups=mesh['stn'=4,'chan'=64] {'stn','chan'}, dimensions={0} | all-to-all | bytes 8388608 | tf_op jit(solution)/shard_map/all_to_all | solution.py:241
  215.0 18.1 %shard_map.38 = bf16[4,2,256,1024]{3,2,1,0:T(8,128)(2,1)} custom-call(bf16[1024,16,128]{2,1,0:T(8,128)(2,1)} %all_to_all.15.refs_0_), custom_call_target="tpu_custom_call" | custom-call | flops 8999999488 | bytes 8388608 | tf_op jit(solution)/shard_map/pallas_call | solution.py:213
  233.0 99.5 %all_to_all.16 = bf16[4,2,256,1024]{3,2,1,0:T(8,128)(2,1)S(1)} all-to-all(bf16[4,2,256,1024]{3,2,1,0:T(8,128)(2,1)} %shard_map.38), channel_id=1, replica_groups=mesh['stn'=4,'chan'=64] {'stn'}, dimensions={0} | all-to-all | bytes 8388608 | tf_op jit(solution)/shard_map/all_to_all | solution.py:244
  332.5 4.4 %bitcast_convert_fusion = f32[4,1,2,256,1024]{4,3,2,1,0:T(8,128)} fusion(bf16[4,2,256,1024]{3,2,1,0:T(8,128)(2,1)S(1)} %all_to_all.16), kind=kLoop, calls=%fused_computation | loop fusion | flops 2097152 | bytes 12582912 | tf_op jit(solution)/shard_map/broadcast_in_dim | solution.py:245
Async XLA Ops:
  0.0 59.0 %all-to-all-start = ((bf16[256,8,1024]{2,1,0:T(8,128)(2,1)}), bf16[256,8,1024]{2,1,0:T(8,128)(2,1)}, u32[]{:S(2)}, u32[]{:S(2)}) async-start(bf16[256,8,1024]{2,1,0:T(8,128)(2,1)} %bitcast.9), calls=%async_computation | async-start | bytes 8388608 | tf_op jit(solution)/shard_map/all_to_all | solution.py:237

commit v2 on v1

v2 whole, which is shorter than its diff:
```python
import math

import jax
import jax.numpy as jnp
import numpy as np
from jax import lax
from jax.experimental import pallas as pl
from jax.experimental.pallas import tpu as pltpu
from jax.sharding import PartitionSpec as P

AVG = 16
LANES = 128


def dft_table(slots, par):
    half = slots // 2
    q = 2 * np.arange(half, dtype=np.int64) + par
    turns = (q[:, None] * np.arange(half, dtype=np.int64)) % slots
    angles = turns.astype(np.float64) * (-2.0 * math.pi / slots)
    table = np.concatenate([np.cos(angles), np.sin(angles)]).astype(np.float32)
    upper = table.astype(jnp.bfloat16)
    lower = (table - upper.astype(np.float32)).astype(jnp.bfloat16)
    return np.concatenate([upper, lower], axis=1)


def first_twist(slots, phases, par):
    half = slots // 2
    q = 2 * jnp.arange(half, dtype=jnp.int32) + par
    q = jnp.broadcast_to(q[:, None], (half, LANES))
    angles = q.astype(jnp.float32) * jnp.float32(-2.0 * math.pi / (phases * slots))
    return jnp.stack([jnp.cos(angles), jnp.sin(angles)])


def transform(phase, g, tab_ref, t1_ref, br, tw):
    rows, half = g.shape[0], g.shape[1] // 2
    dims = (((1,), (1,)), ((), ()))

    @pl.when(phase == 0)
    def _():
        tw[0] = jnp.ones(tw.shape[1:], jnp.float32)
        tw[1] = jnp.zeros(tw.shape[1:], jnp.float32)

    def product(table, values):
        return lax.dot_general(table, values, dims, preferred_element_type=jnp.float32)

    upper, lower = g[:, :half], g[:, half:]
    both = (
        product(tab_ref[:, :half], upper)
        + product(tab_ref[:, half:], upper)
        + product(tab_ref[:, :half], lower)
    )
    cos, sin = tw[0], tw[1]
    for part in range(rows // LANES):
        re = both[:half, part * LANES : (part + 1) * LANES]
        im = both[half:, part * LANES : (part + 1) * LANES]
        br[phase, 0, part] = (re * cos - im * sin).astype(jnp.bfloat16)
        br[phase, 1, part] = (re * sin + im * cos).astype(jnp.bfloat16)
    tw[0] = cos * t1_ref[0] - sin * t1_ref[1]
    tw[1] = cos * t1_ref[1] + sin * t1_ref[0]


def bands(frames, br, o_ref, start, emit):
    phases, _, parts, half, _ = br.shape
    root = math.sqrt(0.5)
    tile = 16
    count = half // tile
    left = lax.broadcasted_iota(jnp.int32, (tile, LANES), 1) < frames

    def four(a, b, c, d):
        (ar, ai), (b_r, bi), (cr, ci), (dr, di) = a, b, c, d
        er, ei, fr_, fi = ar + cr, ai + ci, ar - cr, ai - ci
        gr, gi, hr, hi = b_r + dr, bi + di, b_r - dr, bi - di
        return ((er + gr, ei + gi), (fr_ + hi, fi - hr), (er - gr, ei - gi), (fr_ - hi, fi + hr))

    @pl.loop(0, count)
    def _(step):
        block = lax.rem(start + step, count)
        at = pl.multiple_of(block * tile, tile)
        for part in range(parts):
            b = [
                tuple(br[p, ri, part, pl.ds(at, tile), :].astype(jnp.float32) for ri in range(2))
                for p in range(8)
            ]
            even = four(b[0], b[2], b[4], b[6])
            odd = four(b[1], b[3], b[5], b[7])
            (o1r, o1i), (o2r, o2i), (o3r, o3i) = odd[1:]
            turned = (
                odd[0],
                ((o1r + o1i) * root, (o1i - o1r) * root),
                (o2i, -o2r),
                ((o3i - o3r) * root, (-o3r - o3i) * root),
            )
            for c in range(4):
                re = even[c][0] + turned[c][0]
                im = even[c][1] + turned[c][1]
                first = jnp.where(left, re, pltpu.roll(im, frames, 1)).reshape(2, 8, LANES)
                second = jnp.where(left, pltpu.roll(re, frames, 1), im).reshape(2, 8, LANES)
                both = jnp.concatenate([first, second], axis=1)
                o_ref[c, pl.ds(block * 2, 2), part] = both.astype(jnp.bfloat16)

        @pl.when(step > 0)
        def _():
            emit(lax.rem(start + step + count - 1, count))

    emit(lax.rem(start + count - 1, count))


def channelise_kernel(
    spectra_count, a_ref, fir_ref, tab_ref, t1_ref, r0_ref, r1_ref, xs, g, later, br, tw, out, send_sem, recv_sem
):
    phase = pl.program_id(0)
    groups, _, inputs, fr, slots = a_ref.shape
    frames = groups * fr
    taps = fir_ref.shape[1]
    half = slots // 2
    stations, spans = out.shape[1], out.shape[2]
    my_stn, my_chan = lax.axis_index("stn"), lax.axis_index("chan")
    me = my_stn * spans + my_chan

    @pl.when(phase == 0)
    def _():
        xs[:, :, frames:, :] = jnp.zeros((inputs, slots // LANES, xs.shape[2] - frames, LANES), jnp.float32)

    for i in range(inputs):
        for grp in range(groups):
            line = a_ref[grp, 0, i].astype(jnp.float32)
            for col in range(slots // LANES):
                xs[i, col, grp * fr : (grp + 1) * fr, :] = line[:, col * LANES : (col + 1) * LANES]

    keep = lax.broadcasted_iota(jnp.int32, (frames, LANES), 0) < spectra_count

    @pl.loop(0, inputs)
    def _(i):
        for chunk in range(half // LANES):

            def fir(at):
                total = None
                for k in range(taps):
                    term = fir_ref[0, k : k + 1, at : at + LANES] * xs[
                        i, at // LANES, taps - 1 - k : taps - 1 - k + frames, :
                    ]
                    total = term if total is None else total + term
                return jnp.where(keep, total, 0.0)

            at = chunk * LANES
            low, high = fir(at), fir(at + half)
            row = pl.multiple_of(i * frames, frames)

            def keep_split(value, store):
                upper = value.astype(jnp.bfloat16)
                store(at, upper)
                store(half + at, (value - upper.astype(jnp.float32)).astype(jnp.bfloat16))

            def now(lane, value):
                g[pl.ds(row, frames), lane : lane + LANES] = value

            def after(lane, value):
                later[phase, pl.ds(row, frames), lane : lane + LANES] = value

            keep_split(low + high, now)
            keep_split(low - high, after)

    transform(phase, g, tab_ref.at[0], t1_ref.at[0], br, tw)

    def emit(par, target):
        def blocks(block):
            for turn in range(2):
                u = 2 * block + lax.rem(my_chan + turn, 2)
                for shift in range(stations):
                    c = lax.rem(my_stn + shift, stations)
                    source, landing = out.at[par, c, u], target.at[me]
                    mine = jnp.logical_and(shift == 0, u == my_chan)

                    @pl.when(mine)
                    def _():
                        pltpu.make_async_copy(source, landing, recv_sem.at[par]).start()

                    @pl.when(jnp.logical_not(mine))
                    def _():
                        pltpu.make_async_remote_copy(
                            src_ref=source,
                            dst_ref=landing,
                            send_sem=send_sem.at[par],
                            recv_sem=recv_sem.at[par],
                            device_id=(c, u),
                            device_id_type=pl.DeviceIdType.MESH,
                        ).start()

        return blocks

    @pl.when(phase == pl.num_programs(0) - 1)
    def _():
        start = my_chan // 2
        bands(frames, br, out.at[0], start, emit(0, r0_ref))

        @pl.loop(0, later.shape[0])
        def _(p):
            transform(p, later.at[p], tab_ref.at[1], t1_ref.at[1], br, tw)

        bands(frames, br, out.at[1], start, emit(1, r1_ref))
        for par, target in ((0, r0_ref), (1, r1_ref)):
            pltpu.make_async_copy(target, target, recv_sem.at[par]).wait()
            others = target.at[pl.ds(0, stations * spans - 1)]
            pltpu.make_async_copy(others, others, send_sem.at[par]).wait()


def channelise(samples, fir_taps, spectra_count, stations):
    groups, phases, inputs, fr, slots = samples.shape
    frames = groups * fr
    taps = fir_taps.shape[1]
    half = slots // 2
    rows = inputs * frames
    parts = rows // LANES
    spans = slots // AVG
    whole = pl.BlockSpec(memory_space=pltpu.VMEM)
    landing = jax.ShapeDtypeStruct((stations * spans, parts, AVG, LANES), jnp.bfloat16)
    table = np.stack([dft_table(slots, par) for par in range(2)])
    twist = jnp.stack([first_twist(slots, phases, par) for par in range(2)])
    return pl.pallas_call(
        lambda *refs: channelise_kernel(spectra_count, *refs),
        grid=(phases,),
        out_shape=(landing, landing),
        in_specs=[
            pl.BlockSpec((groups, 1, inputs, fr, slots), lambda p: (0, p, 0, 0, 0)),
            pl.BlockSpec((1, taps, slots), lambda p: (p, 0, 0)),
            whole,
            whole,
        ],
        out_specs=[pl.BlockSpec(memory_space=pl.ANY)] * 2,
        scratch_shapes=[
            pltpu.VMEM((inputs, slots // LANES, frames + 8, LANES), jnp.float32),
            pltpu.VMEM((rows, slots), jnp.bfloat16),
            pltpu.VMEM((phases, rows, slots), jnp.bfloat16),
            pltpu.VMEM((phases, 2, parts, half, LANES), jnp.bfloat16),
            pltpu.VMEM((2, half, LANES), jnp.float32),
            pltpu.VMEM((2, stations, spans, parts, AVG, LANES), jnp.bfloat16),
            pltpu.SemaphoreType.DMA((2,)),
            pltpu.SemaphoreType.DMA((2,)),
        ],
        compiler_params=pltpu.CompilerParams(vmem_limit_bytes=60 << 20, has_side_effects=True),
        cost_estimate=pl.CostEstimate(flops=20 * 10**9, bytes_accessed=20 << 20, transcendentals=0),
    )(samples, fir_taps, jnp.asarray(table), twist)


def correlate_kernel(scaling, r0_ref, r1_ref, o_ref, wide, x, y):
    inputs, lanes = x.shape[0], LANES
    items = x.shape[1] // lanes // 2
    sub = wide.shape[0] // items
    tiles = sub * items // AVG
    dims = (((1,), (1,)), ((), ()))

    @pl.when(pl.program_id(0) == 0)
    def _():
        for par, r_ref in ((0, r0_ref), (1, r1_ref)):

            @pl.loop(0, inputs // sub)
            def _(block):
                row = pl.multiple_of(block * sub, sub)
                at = pl.multiple_of(block * tiles, tiles)
                wide[...] = r_ref[pl.ds(at, tiles)].astype(jnp.float32).reshape(sub * items, lanes)
                left = lax.broadcasted_iota(jnp.int32, (sub, lanes), 1) < lanes // 2
                for item in range(items):
                    value = wide[pl.ds(item, sub, stride=items), :]
                    turned = pltpu.roll(value, lanes // 2, 1)
                    lane = (par * items + item) * lanes
                    x[pl.ds(row, sub), lane : lane + lanes] = value.astype(jnp.bfloat16)
                    y[pl.ds(row, sub), lane : lane + lanes] = jnp.where(left, turned, -turned).astype(jnp.bfloat16)

    rows = o_ref.shape[2]
    at = pl.multiple_of(pl.program_id(0) * rows, rows)
    for part, source in ((0, x), (1, y)):
        product = lax.dot_general(source[pl.ds(at, rows), :], x[...], dims, preferred_element_type=jnp.float32)
        o_ref[0, part] = (product * scaling).astype(o_ref.dtype)


def correlate(first, second, scaling, inputs):
    items = first.shape[0] * AVG // inputs
    rows = 256
    whole = pl.BlockSpec(memory_space=pltpu.VMEM)
    return pl.pallas_call(
        lambda *refs: correlate_kernel(scaling, *refs),
        grid=(inputs // rows,),
        out_shape=jax.ShapeDtypeStruct((inputs // rows, 2, rows, inputs), jnp.bfloat16),
        in_specs=[whole, whole],
        out_specs=pl.BlockSpec((1, 2, rows, inputs), lambda j: (j, 0, 0, 0)),
        scratch_shapes=[
            pltpu.VMEM((128 * items, LANES), jnp.float32),
            pltpu.VMEM((inputs, 2 * items * LANES), jnp.bfloat16),
            pltpu.VMEM((inputs, 2 * items * LANES), jnp.bfloat16),
        ],
        compiler_params=pltpu.CompilerParams(vmem_limit_bytes=60 << 20),
        cost_estimate=pl.CostEstimate(flops=9 * 10**9, bytes_accessed=12 << 20, transcendentals=0),
    )(first, second)


def per_device(voltages, fir_taps):
    inputs_dev, _, fr, slots = voltages.shape
    phases, taps, _ = fir_taps.shape
    lane_count = lax.axis_size("chan")
    stations = lax.axis_size("stn")
    groups = lane_count // phases
    own = inputs_dev // lane_count
    frames = groups * fr
    spectra_count = frames - (taps - 1)
    dealt = lax.all_to_all(voltages[:, 0], "chan", 0, 0, tiled=True)
    samples = dealt.reshape(groups, phases, own, fr, slots)
    first, second = channelise(samples, fir_taps, spectra_count, stations)
    inputs = inputs_dev * stations
    scaling = 1.0 / (phases * slots * AVG * spectra_count)
    rows = correlate(first.reshape(-1, AVG, LANES), second.reshape(-1, AVG, LANES), scaling, inputs)
    mine = lax.all_to_all(rows, "stn", 0, 0, tiled=True)
    return mine.astype(jnp.float32)[:, None]


def solution(mesh):
    return jax.shard_map(
        per_device,
        mesh=mesh,
        in_specs=(P("stn", "chan", None, None), P()),
        out_specs=P(None, "chan", None, "stn", None),
        check_vma=False,
    )
```

time: 337 us -> 311 us (0.923)
  the two profiles are of different devices: /device:TPU:24 before, /device:TPU:3 now
where the time goes in v2:
time: 311 us; the launch traced here: 310 us
  Pallas kernels  146 us (47%)
  blocking collectives  98.6 us (32%)
  waiting for transfers between devices  49.3 us (16%)
  starting transfers between devices  9.85 us (3%)
  other arithmetic  5.73 us (2%)
    pallas_call x1, Pallas kernels, channelise(): pl.pallas_call(lambda *refs: channelise_kernel(spectra_count, *refs), gri...  129 us
    all_to_all x1, blocking collectives, per_device(): mine = lax.all_to_all(rows, 'stn', 0, 0, tiled=True)  98.6 us
    all_to_all x1, waiting for transfers between devices, per_device(): dealt = lax.all_to_all(voltages[:, 0], 'chan', 0, 0, tiled=True)  49.3 us
    pallas_call x1, Pallas kernels, correlate(): pl.pallas_call(lambda *refs: correlate_kernel(scaling, *refs), grid=(inpu...  17 us
    all_to_all x1, starting transfers between devices, per_device(): dealt = lax.all_to_all(voltages[:, 0], 'chan', 0, 0, tiled=True)  9.85 us
  transfers between devices with their start and end apart: 1, of which 1 were waited for; matrix products, arithmetic and copies ran while one was open for 1% of the time, Pallas kernels for 0%

profile of v2, /device:TPU:3, one launch (start us, length us, event | category | flops | bytes accessed | tf_op | source)
XLA Modules:
  0.0 309.9 jit_solution(5347423021015237522)
XLA Ops:
  0.0 9.9 %all-to-all-start = ((bf16[256,8,1024]{2,1,0:T(8,128)(2,1)}), bf16[256,8,1024]{2,1,0:T(8,128)(2,1)}, u32[]{:S(2)}, u32[]{:S(2)}) async-start(bf16[256,8,1024]{2,1,0:T(8,128)(2,1)} %bitcast.14), calls=%async_computation | async-start | bytes 8388608 | tf_op jit(solution)/shard_map/all_to_all | solution.py:305
  10.1 0.1 broadcast_in_dim.23
  10.2 0.1 broadcast_in_dim.22
  10.3 0.1 broadcast_in_dim.25
  10.5 0.1 broadcast_in_dim.24
  10.6 0.1 maximum_bitcast_fusion
  10.7 1.0 pad_maximum_fusion.refs_3_
  11.7 49.3 %all-to-all-done = bf16[256,8,1024]{2,1,0:T(8,128)(2,1)} async-done(((bf16[256,8,1024]{2,1,0:T(8,128)(2,1)}), bf16[256,8,1024]{2,1,0:T(8,128)(2,1)}, u32[]{:S(2)}, u32[]{:S(2)}) %all-to-all-start) | async-done | bytes 4194336 | tf_op jit(solution)/shard_map/all_to_all | solution.py:305
  61.0 128.8 %shard_map.37 = (bf16[256,2,16,128]{3,2,1,0:T(8,128)(2,1)}, bf16[256,2,16,128]{3,2,1,0:T(8,128)(2,1)}) custom-call(bf16[8,8,4,8,1024]{4,3,2,1,0:T(8,128)(2,1)} %bitcast.1.refs_0_, f32[8,8,1024]{2,1,0:T(8,128)} %refs_1_.1, bf16[2,1024,1024]{2,1,0:T(8,128)(2,1)} %constant.8.clone.refs_2_, f32[2,2,512,128]{3,2,1,0:T(8,128)} %pad_maximum_fusion.refs_3_), custom_call_target="tpu_custom_call" | custom-call | flops 20000000000 | bytes 20971520 | tf_op jit(solution)/shard_map/pallas_call | solution.py:219
  189.8 17.0 %shard_map.38 = bf16[4,2,256,1024]{3,2,1,0:T(8,128)(2,1)} custom-call(bf16[512,16,128]{2,1,0:T(8,128)(2,1)} %bitcast.15, bf16[512,16,128]{2,1,0:T(8,128)(2,1)} %bitcast.16), custom_call_target="tpu_custom_call" | custom-call | flops 8999999488 | bytes 12582912 | tf_op jit(solution)/shard_map/pallas_call | solution.py:280
  206.9 98.6 %all_to_all.10 = bf16[4,2,256,1024]{3,2,1,0:T(8,128)(2,1)S(1)} all-to-all(bf16[4,2,256,1024]{3,2,1,0:T(8,128)(2,1)} %shard_map.38), channel_id=1, replica_groups=mesh['stn'=4,'chan'=64] {'stn'}, dimensions={0} | all-to-all | bytes 8388608 | tf_op jit(solution)/shard_map/all_to_all | solution.py:311
  305.4 4.4 %bitcast_convert_fusion = f32[4,1,2,256,1024]{4,3,2,1,0:T(8,128)} fusion(bf16[4,2,256,1024]{3,2,1,0:T(8,128)(2,1)S(1)} %all_to_all.10), kind=kLoop, calls=%fused_computation | loop fusion | flops 2097152 | bytes 12582912 | tf_op jit(solution)/shard_map/broadcast_in_dim | solution.py:312
  (4 shorter events, 0.2 us)
Async XLA Ops:
  0.0 61.0 %all-to-all-start = ((bf16[256,8,1024]{2,1,0:T(8,128)(2,1)}), bf16[256,8,1024]{2,1,0:T(8,128)(2,1)}, u32[]{:S(2)}, u32[]{:S(2)}) async-start(bf16[256,8,1024]{2,1,0:T(8,128)(2,1)} %bitcast.14), calls=%async_computation | async-start | bytes 8388608 | tf_op jit(solution)/shard_map/all_to_all | solution.py:305

commit v3 on v2

--- a/solution.py
+++ b/solution.py
@@ -105,8 +105,50 @@
     emit(lax.rem(start + count - 1, count))
 
 
+def spread(r_ref, wide, x, y):
+    inputs, lanes = x.shape[0], LANES
+    items = x.shape[1] // lanes
+    sub = wide.shape[0] // items
+    tiles = sub * items // AVG
+
+    @pl.loop(0, inputs // sub)
+    def _(block):
+        row = pl.multiple_of(block * sub, sub)
+        at = pl.multiple_of(block * tiles, tiles)
+        wide[...] = r_ref[pl.ds(at, tiles)].astype(jnp.float32).reshape(sub * items, lanes)
+        left = lax.broadcasted_iota(jnp.int32, (sub, lanes), 1) < lanes // 2
+        for item in range(items):
+            value = wide[pl.ds(item, sub, stride=items), :]
+            turned = pltpu.roll(value, lanes // 2, 1)
+            lane = item * lanes
+            x[pl.ds(row, sub), lane : lane + lanes] = value.astype(jnp.bfloat16)
+            y[pl.ds(row, sub), lane : lane + lanes] = jnp.where(left, turned, -turned).astype(jnp.bfloat16)
+
+
 def channelise_kernel(
-    spectra_count, a_ref, fir_ref, tab_ref, t1_ref, r0_ref, r1_ref, xs, g, later, br, tw, out, send_sem, recv_sem
+    spectra_count,
+    scaling,
+    a_ref,
+    fir_ref,
+    tab_ref,
+    t1_ref,
+    v_ref,
+    xs,
+    g,
+    later,
+    br,
+    tw,
+    out,
+    landed,
+    wide,
+    x,
+    y,
+    partial,
+    rows_out,
+    send_sem,
+    recv_sem,
+    row_send,
+    row_recv,
 ):
     phase = pl.program_id(0)
     groups, _, inputs, fr, slots = a_ref.shape
@@ -162,13 +204,16 @@
 
     transform(phase, g, tab_ref.at[0], t1_ref.at[0], br, tw)
 
-    def emit(par, target):
+    slots_each = landed.shape[1] // (stations * spans)
+
+    def emit(par):
         def blocks(block):
             for turn in range(2):
                 u = 2 * block + lax.rem(my_chan + turn, 2)
                 for shift in range(stations):
                     c = lax.rem(my_stn + shift, stations)
-                    source, landing = out.at[par, c, u], target.at[me]
+                    source = out.at[par, c, u]
+                    landing = landed.at[par, pl.ds(me * slots_each, slots_each)]
                     mine = jnp.logical_and(shift == 0, u == my_chan)
 
                     @pl.when(mine)
@@ -191,20 +236,83 @@
     @pl.when(phase == pl.num_programs(0) - 1)
     def _():
         start = my_chan // 2
-        bands(frames, br, out.at[0], start, emit(0, r0_ref))
+        bands(frames, br, out.at[0], start, emit(0))
 
         @pl.loop(0, later.shape[0])
         def _(p):
             transform(p, later.at[p], tab_ref.at[1], t1_ref.at[1], br, tw)
 
-        bands(frames, br, out.at[1], start, emit(1, r1_ref))
-        for par, target in ((0, r0_ref), (1, r1_ref)):
-            pltpu.make_async_copy(target, target, recv_sem.at[par]).wait()
-            others = target.at[pl.ds(0, stations * spans - 1)]
+        bands(frames, br, out.at[1], start, emit(1))
+
+        dims = (((1,), (1,)), ((), ()))
+        height = rows_out.shape[2]
+
+        def product(j, part):
+            source = (x, y)[part]
+            at = pl.multiple_of(j * height, height)
+            return lax.dot_general(source[pl.ds(at, height), :], x[...], dims, preferred_element_type=jnp.float32)
+
+        def arrived(par):
+            pltpu.make_async_copy(landed.at[par], landed.at[par], recv_sem.at[par]).wait()
+
+        arrived(0)
+        spread(landed.at[0], wide, x, y)
+
+        @pl.loop(0, stations)
+        def _(j):
+            for part in range(2):
+                partial[j, part] = product(j, part)
+
+        arrived(1)
+        spread(landed.at[1], wide, x, y)
+
+        def owner(turn):
+            return lax.rem(my_stn + jnp.where(turn < 2, 2 + turn, 3 - turn), stations)
+
+        def send(j, part):
+            source, landing = rows_out.at[j, part], v_ref.at[my_stn, part]
+
+            @pl.when(j == my_stn)
+            def _():
+                pltpu.make_async_copy(source, landing, row_recv).start()
+
+            @pl.when(j != my_stn)
+            def _():
+                pltpu.make_async_remote_copy(
+                    src_ref=source,
+                    dst_ref=landing,
+                    send_sem=row_send,
+                    recv_sem=row_recv,
+                    device_id=(j, my_chan),
+                    device_id_type=pl.DeviceIdType.MESH,
+                ).start()
+
+        def finish(j, part):
+            total = (partial[j, part] + product(j, part)) * scaling
+            rows_out[j, part] = total.astype(rows_out.dtype)
+
+        @pl.loop(0, stations)
+        def _(turn):
+            j = owner(turn)
+            finish(j, 0)
+
+            @pl.when(turn > 0)
+            def _():
+                send(owner(turn - 1), 1)
+
+            finish(j, 1)
+            send(j, 0)
+
+        send(owner(stations - 1), 1)
+        for par in range(2):
+            others = landed.at[par, pl.ds(0, landed.shape[1] - slots_each)]
             pltpu.make_async_copy(others, others, send_sem.at[par]).wait()
-
-
-def channelise(samples, fir_taps, spectra_count, stations):
+        pltpu.make_async_copy(v_ref, v_ref, row_recv).wait()
+        others = v_ref.at[pl.ds(0, stations - 1)]
+        pltpu.make_async_copy(others, others, row_send).wait()
+
+
+def correlate(samples, fir_taps, spectra_count, scaling, stations, rows_dev):
     groups, phases, inputs, fr, slots = samples.shape
     frames = groups * fr
     taps = fir_taps.shape[1]
@@ -213,20 +321,21 @@
     parts = rows // LANES
     spans = slots // AVG
     whole = pl.BlockSpec(memory_space=pltpu.VMEM)
-    landing = jax.ShapeDtypeStruct((stations * spans, parts, AVG, LANES), jnp.bfloat16)
+    whole_inputs = stations * rows_dev
+    depth = AVG // 2 * LANES
     table = np.stack([dft_table(slots, par) for par in range(2)])
     twist = jnp.stack([first_twist(slots, phases, par) for par in range(2)])
     return pl.pallas_call(
-        lambda *refs: channelise_kernel(spectra_count, *refs),
+        lambda *refs: channelise_kernel(spectra_count, scaling, *refs),
         grid=(phases,),
-        out_shape=(landing, landing),
+        out_shape=jax.ShapeDtypeStruct((stations, 2, rows_dev, whole_inputs), jnp.bfloat16),
         in_specs=[
             pl.BlockSpec((groups, 1, inputs, fr, slots), lambda p: (0, p, 0, 0, 0)),
             pl.BlockSpec((1, taps, slots), lambda p: (p, 0, 0)),
             whole,
             whole,
         ],
-        out_specs=[pl.BlockSpec(memory_space=pl.ANY)] * 2,
+        out_specs=pl.BlockSpec(memory_space=pl.ANY),
         scratch_shapes=[
             pltpu.VMEM((inputs, slots // LANES, frames + 8, LANES), jnp.float32),
             pltpu.VMEM((rows, slots), jnp.bfloat16),
@@ -234,63 +343,20 @@
             pltpu.VMEM((phases, 2, parts, half, LANES), jnp.bfloat16),
             pltpu.VMEM((2, half, LANES), jnp.float32),
             pltpu.VMEM((2, stations, spans, parts, AVG, LANES), jnp.bfloat16),
+            pltpu.VMEM((2, stations * spans * parts, AVG, LANES), jnp.bfloat16),
+            pltpu.VMEM((LANES * AVG // 2, LANES), jnp.float32),
+            pltpu.VMEM((whole_inputs, depth), jnp.bfloat16),
+            pltpu.VMEM((whole_inputs, depth), jnp.bfloat16),
+            pltpu.VMEM((stations, 2, rows_dev, whole_inputs), jnp.float32),
+            pltpu.VMEM((stations, 2, rows_dev, whole_inputs), jnp.bfloat16),
             pltpu.SemaphoreType.DMA((2,)),
             pltpu.SemaphoreType.DMA((2,)),
+            pltpu.SemaphoreType.DMA,
+            pltpu.SemaphoreType.DMA,
         ],
         compiler_params=pltpu.CompilerParams(vmem_limit_bytes=60 << 20, has_side_effects=True),
-        cost_estimate=pl.CostEstimate(flops=20 * 10**9, bytes_accessed=20 << 20, transcendentals=0),
+        cost_estimate=pl.CostEstimate(flops=30 * 10**9, bytes_accessed=20 << 20, transcendentals=0),
     )(samples, fir_taps, jnp.asarray(table), twist)
-
-
-def correlate_kernel(scaling, r0_ref, r1_ref, o_ref, wide, x, y):
-    inputs, lanes = x.shape[0], LANES
-    items = x.shape[1] // lanes // 2
-    sub = wide.shape[0] // items
-    tiles = sub * items // AVG
-    dims = (((1,), (1,)), ((), ()))
-
-    @pl.when(pl.program_id(0) == 0)
-    def _():
-        for par, r_ref in ((0, r0_ref), (1, r1_ref)):
-
-            @pl.loop(0, inputs // sub)
-            def _(block):
-                row = pl.multiple_of(block * sub, sub)
-                at = pl.multiple_of(block * tiles, tiles)
-                wide[...] = r_ref[pl.ds(at, tiles)].astype(jnp.float32).reshape(sub * items, lanes)
-                left = lax.broadcasted_iota(jnp.int32, (sub, lanes), 1) < lanes // 2
-                for item in range(items):
-                    value = wide[pl.ds(item, sub, stride=items), :]
-                    turned = pltpu.roll(value, lanes // 2, 1)
-                    lane = (par * items + item) * lanes
-                    x[pl.ds(row, sub), lane : lane + lanes] = value.astype(jnp.bfloat16)
-                    y[pl.ds(row, sub), lane : lane + lanes] = jnp.where(left, turned, -turned).astype(jnp.bfloat16)
-
-    rows = o_ref.shape[2]
-    at = pl.multiple_of(pl.program_id(0) * rows, rows)
-    for part, source in ((0, x), (1, y)):
-        product = lax.dot_general(source[pl.ds(at, rows), :], x[...], dims, preferred_element_type=jnp.float32)
-        o_ref[0, part] = (product * scaling).astype(o_ref.dtype)
-
-
-def correlate(first, second, scaling, inputs):
-    items = first.shape[0] * AVG // inputs
-    rows = 256
-    whole = pl.BlockSpec(memory_space=pltpu.VMEM)
-    return pl.pallas_call(
-        lambda *refs: correlate_kernel(scaling, *refs),
-        grid=(inputs // rows,),
-        out_shape=jax.ShapeDtypeStruct((inputs // rows, 2, rows, inputs), jnp.bfloat16),
-        in_specs=[whole, whole],
-        out_specs=pl.BlockSpec((1, 2, rows, inputs), lambda j: (j, 0, 0, 0)),
-        scratch_shapes=[
-            pltpu.VMEM((128 * items, LANES), jnp.float32),
-            pltpu.VMEM((inputs, 2 * items * LANES), jnp.bfloat16),
-            pltpu.VMEM((inputs, 2 * items * LANES), jnp.bfloat16),
-        ],
-        compiler_params=pltpu.CompilerParams(vmem_limit_bytes=60 << 20),
-        cost_estimate=pl.CostEstimate(flops=9 * 10**9, bytes_accessed=12 << 20, transcendentals=0),
-    )(first, second)
 
 
 def per_device(voltages, fir_taps):
@@ -304,11 +370,8 @@
     spectra_count = frames - (taps - 1)
     dealt = lax.all_to_all(voltages[:, 0], "chan", 0, 0, tiled=True)
     samples = dealt.reshape(groups, phases, own, fr, slots)
-    first, second = channelise(samples, fir_taps, spectra_count, stations)
-    inputs = inputs_dev * stations
     scaling = 1.0 / (phases * slots * AVG * spectra_count)
-    rows = correlate(first.reshape(-1, AVG, LANES), second.reshape(-1, AVG, LANES), scaling, inputs)
-    mine = lax.all_to_all(rows, "stn", 0, 0, tiled=True)
+    mine = correlate(samples, fir_taps, spectra_count, scaling, stations, inputs_dev)
     return mine.astype(jnp.float32)[:, None]
 
 

time: 311 us -> 293 us (0.942)
  blocking collectives: 98.6 us -> 0 us
  Pallas kernels: 146 us -> 224 us
    all_to_all x1 -> x0, blocking collectives: 98.6 us -> none  [per_device(): mine = lax.all_to_all(rows, 'stn', 0, 0, tiled=True)]
    pallas_call x2 -> x1, Pallas kernels: 146 us -> 224 us  [correlate(): pl.pallas_call(lambda *refs: channelise_kernel(spectra_count, scaling, *r...]
where the time goes in v3:
time: 293 us; the launch traced here: 291 us
  Pallas kernels  224 us (76%)
  waiting for transfers between devices  49.3 us (17%)
  starting transfers between devices  9.85 us (3%)
  other arithmetic  7.93 us (3%)
    pallas_call x1, Pallas kernels, correlate(): pl.pallas_call(lambda *refs: channelise_kernel(spectra_count, scaling, *r...  224 us
    all_to_all x1, waiting for transfers between devices, per_device(): dealt = lax.all_to_all(voltages[:, 0], 'chan', 0, 0, tiled=True)  49.3 us
    all_to_all x1, starting transfers between devices, per_device(): dealt = lax.all_to_all(voltages[:, 0], 'chan', 0, 0, tiled=True)  9.85 us
    broadcast_in_dim x1, other arithmetic, per_device(): return mine.astype(jnp.float32)[:, None]  6.64 us
  transfers between devices with their start and end apart: 1, of which 1 were waited for; matrix products, arithmetic and copies ran while one was open for 1% of the time, Pallas kernels for 0%

profile of v3, /device:TPU:3, one launch (start us, length us, event | category | flops | bytes accessed | tf_op | source)
XLA Modules:
  0.0 291.4 jit_solution(11465231769486362047)
XLA Ops:
  0.0 9.9 %all-to-all-start = ((bf16[256,8,1024]{2,1,0:T(8,128)(2,1)}), bf16[256,8,1024]{2,1,0:T(8,128)(2,1)}, u32[]{:S(2)}, u32[]{:S(2)}) async-start(bf16[256,8,1024]{2,1,0:T(8,128)(2,1)} %bitcast.12), calls=%async_computation | async-start | bytes 8388608 | tf_op jit(solution)/shard_map/all_to_all | solution.py:371
  10.1 0.1 broadcast_in_dim.23
  10.2 0.1 broadcast_in_dim.22
  10.3 0.1 broadcast_in_dim.25
  10.5 0.1 broadcast_in_dim.24
  10.6 0.1 maximum_bitcast_fusion
  10.7 1.0 pad_maximum_fusion.refs_3_
  11.7 49.3 %all-to-all-done = bf16[256,8,1024]{2,1,0:T(8,128)(2,1)} async-done(((bf16[256,8,1024]{2,1,0:T(8,128)(2,1)}), bf16[256,8,1024]{2,1,0:T(8,128)(2,1)}, u32[]{:S(2)}, u32[]{:S(2)}) %all-to-all-start) | async-done | bytes 4194336 | tf_op jit(solution)/shard_map/all_to_all | solution.py:371
  61.0 223.8 %shard_map.37 = bf16[4,2,256,1024]{3,2,1,0:T(8,128)(2,1)} custom-call(bf16[8,8,4,8,1024]{4,3,2,1,0:T(8,128)(2,1)} %bitcast.1.refs_0_, f32[8,8,1024]{2,1,0:T(8,128)} %refs_1_.1, bf16[2,1024,1024]{2,1,0:T(8,128)(2,1)} %constant.8.clone.refs_2_, f32[2,2,512,128]{3,2,1,0:T(8,128)} %pad_maximum_fusion.refs_3_), custom_call_target="tpu_custom_call" | custom-call | flops 30000001024 | bytes 20971520 | tf_op jit(solution)/shard_map/pallas_call | solution.py:328
  284.8 6.6 %bitcast_convert_fusion = f32[4,1,2,256,1024]{4,3,2,1,0:T(8,128)} fusion(bf16[4,2,256,1024]{3,2,1,0:T(8,128)(2,1)} %shard_map.37), kind=kLoop, calls=%fused_computation | loop fusion | flops 2097152 | bytes 12582912 | tf_op jit(solution)/shard_map/broadcast_in_dim | solution.py:375
  (4 shorter events, 0.2 us)
Async XLA Ops:
  0.0 61.0 %all-to-all-start = ((bf16[256,8,1024]{2,1,0:T(8,128)(2,1)}), bf16[256,8,1024]{2,1,0:T(8,128)(2,1)}, u32[]{:S(2)}, u32[]{:S(2)}) async-start(bf16[256,8,1024]{2,1,0:T(8,128)(2,1)} %bitcast.12), calls=%async_computation | async-start | bytes 8388608 | tf_op jit(solution)/shard_map/all_to_all | solution.py:371

commit v4 on v3

v4 whole, which is shorter than its diff:
```python
import math

import jax
import jax.numpy as jnp
import numpy as np
from jax import lax
from jax.experimental import pallas as pl
from jax.experimental.pallas import tpu as pltpu
from jax.sharding import PartitionSpec as P

AVG = 16
LANES = 128


def dft_table(slots, par):
    half = slots // 2
    q = 2 * np.arange(half, dtype=np.int64) + par
    turns = (q[:, None] * np.arange(half, dtype=np.int64)) % slots
    angles = turns.astype(np.float64) * (-2.0 * math.pi / slots)
    parts = np.stack([np.cos(angles), np.sin(angles)]).reshape(2, 2, half // 2, half)
    table = parts.transpose(1, 0, 2, 3).reshape(slots, half).astype(np.float32)
    upper = table.astype(jnp.bfloat16)
    lower = (table - upper.astype(np.float32)).astype(jnp.bfloat16)
    return np.concatenate([upper, lower], axis=1)


def first_twist(slots, phases, par):
    half = slots // 2
    q = 2 * jnp.arange(half, dtype=jnp.int32) + par
    q = jnp.broadcast_to(q[:, None], (half, LANES))
    angles = q.astype(jnp.float32) * jnp.float32(-2.0 * math.pi / (phases * slots))
    return jnp.stack([jnp.cos(angles), jnp.sin(angles)])


def transform(phase, at, g, tab_ref, t1_ref, br, tw):
    rows, half = g.shape[0], g.shape[1] // 2
    size = half // 2
    dims = (((1,), (1,)), ((), ()))

    @pl.when(phase == 0)
    def _():
        tw[0] = jnp.ones(tw.shape[1:], jnp.float32)
        tw[1] = jnp.zeros(tw.shape[1:], jnp.float32)

    def product(table, values):
        return lax.dot_general(table, values, dims, preferred_element_type=jnp.float32)

    upper, lower = g[:, :half], g[:, half:]
    both = (
        product(tab_ref[:, :half], upper)
        + product(tab_ref[:, half:], upper)
        + product(tab_ref[:, :half], lower)
    )
    cos, sin = tw[0], tw[1]
    for part in range(rows // LANES):
        re = both[:size, part * LANES : (part + 1) * LANES]
        im = both[size:, part * LANES : (part + 1) * LANES]
        br[phase, 0, part] = (re * cos - im * sin).astype(jnp.bfloat16)
        br[phase, 1, part] = (re * sin + im * cos).astype(jnp.bfloat16)
    first, second = t1_ref[0, pl.ds(at, size), :], t1_ref[1, pl.ds(at, size), :]
    tw[0] = cos * first - sin * second
    tw[1] = cos * second + sin * first


def bands(frames, br, o_ref, base, start, emit):
    phases, _, parts, half, _ = br.shape
    root = math.sqrt(0.5)
    tile = 16
    count = half // tile
    left = lax.broadcasted_iota(jnp.int32, (tile, LANES), 1) < frames

    def four(a, b, c, d):
        (ar, ai), (b_r, bi), (cr, ci), (dr, di) = a, b, c, d
        er, ei, fr_, fi = ar + cr, ai + ci, ar - cr, ai - ci
        gr, gi, hr, hi = b_r + dr, bi + di, b_r - dr, bi - di
        return ((er + gr, ei + gi), (fr_ + hi, fi - hr), (er - gr, ei - gi), (fr_ - hi, fi + hr))

    @pl.loop(0, count)
    def _(step):
        block = lax.rem(start + step, count)
        at = pl.multiple_of(block * tile, tile)
        for part in range(parts):
            b = [
                tuple(br[p, ri, part, pl.ds(at, tile), :].astype(jnp.float32) for ri in range(2))
                for p in range(8)
            ]
            even = four(b[0], b[2], b[4], b[6])
            odd = four(b[1], b[3], b[5], b[7])
            (o1r, o1i), (o2r, o2i), (o3r, o3i) = odd[1:]
            turned = (
                odd[0],
                ((o1r + o1i) * root, (o1i - o1r) * root),
                (o2i, -o2r),
                ((o3i - o3r) * root, (-o3r - o3i) * root),
            )
            for c in range(4):
                re = even[c][0] + turned[c][0]
                im = even[c][1] + turned[c][1]
                first = jnp.where(left, re, pltpu.roll(im, frames, 1)).reshape(2, 8, LANES)
                second = jnp.where(left, pltpu.roll(re, frames, 1), im).reshape(2, 8, LANES)
                both = jnp.concatenate([first, second], axis=1)
                o_ref[c, pl.ds((base + block) * 2, 2), part] = both.astype(jnp.bfloat16)

        @pl.when(step > 0)
        def _():
            emit(base + lax.rem(start + step + count - 1, count))

    emit(base + lax.rem(start + count - 1, count))


def spread(r_ref, wide, x, y):
    inputs, lanes = x.shape[0], LANES
    items = x.shape[1] // lanes
    sub = wide.shape[0] // items
    tiles = sub * items // AVG

    @pl.loop(0, inputs // sub)
    def _(block):
        row = pl.multiple_of(block * sub, sub)
        at = pl.multiple_of(block * tiles, tiles)
        wide[...] = r_ref[pl.ds(at, tiles)].astype(jnp.float32).reshape(sub * items, lanes)
        left = lax.broadcasted_iota(jnp.int32, (sub, lanes), 1) < lanes // 2
        for item in range(items):
            value = wide[pl.ds(item, sub, stride=items), :]
            turned = pltpu.roll(value, lanes // 2, 1)
            lane = item * lanes
            x[pl.ds(row, sub), lane : lane + lanes] = value.astype(jnp.bfloat16)
            y[pl.ds(row, sub), lane : lane + lanes] = jnp.where(left, turned, -turned).astype(jnp.bfloat16)


def channelise_kernel(
    spectra_count,
    scaling,
    volt_ref,
    fir_ref,
    tab_ref,
    t1_ref,
    v_ref,
    inbox,
    xs,
    g,
    br,
    tw,
    out,
    landed,
    wide,
    x,
    y,
    partial,
    rows_out,
    in_send,
    in_recv,
    send_sem,
    recv_sem,
    row_send,
    row_recv,
):
    inputs, lane_count, fr, slots = inbox.shape
    phases, taps, _ = fir_ref.shape
    groups = lane_count // phases
    frames = groups * fr
    half = slots // 2
    stations, spans = out.shape[1], out.shape[2]
    my_stn, my_chan = lax.axis_index("stn"), lax.axis_index("chan")
    me = my_stn * spans + my_chan

    for i in range(inputs):

        @pl.loop(0, lane_count)
        def _(shift):
            lane = lax.rem(my_chan + shift, lane_count)
            source, landing = volt_ref.at[lane * inputs + i], inbox.at[i, my_chan]

            @pl.when(shift == 0)
            def _():
                pltpu.make_async_copy(source, landing, in_recv.at[i]).start()

            @pl.when(shift != 0)
            def _():
                pltpu.make_async_remote_copy(
                    src_ref=source,
                    dst_ref=landing,
                    send_sem=in_send.at[i],
                    recv_sem=in_recv.at[i],
                    device_id=(my_stn, lane),
                    device_id_type=pl.DeviceIdType.MESH,
                ).start()

    xs[:, frames:, :] = jnp.zeros((slots // LANES, xs.shape[1] - frames, LANES), jnp.float32)
    keep = lax.broadcasted_iota(jnp.int32, (frames, LANES), 0) < spectra_count

    @pl.loop(0, inputs)
    def _(i):
        pltpu.make_async_copy(inbox.at[i], inbox.at[i], in_recv.at[i]).wait()
        row = pl.multiple_of(i * frames, frames)

        @pl.loop(0, phases)
        def _(phase):
            for grp in range(groups):
                line = inbox[i, grp * phases + phase].astype(jnp.float32)
                for col in range(slots // LANES):
                    xs[col, grp * fr : (grp + 1) * fr, :] = line[:, col * LANES : (col + 1) * LANES]

            for chunk in range(half // LANES):

                def fir(at):
                    total = None
                    for k in range(taps):
                        term = fir_ref[phase, k : k + 1, at : at + LANES] * xs[
                            at // LANES, taps - 1 - k : taps - 1 - k + frames, :
                        ]
                        total = term if total is None else total + term
                    return jnp.where(keep, total, 0.0)

                at = chunk * LANES
                low, high = fir(at), fir(at + half)
                for par, value in ((0, low + high), (1, low - high)):
                    upper = value.astype(jnp.bfloat16)
                    lower = (value - upper.astype(jnp.float32)).astype(jnp.bfloat16)
                    g[par, phase, pl.ds(row, frames), at : at + LANES] = upper
                    g[par, phase, pl.ds(row, frames), half + at : half + at + LANES] = lower

    slots_each = landed.shape[1] // (stations * spans)

    def emit(par):
        def blocks(block):
            for turn in range(2):
                u = 2 * block + lax.rem(my_chan + turn, 2)
                for shift in range(stations):
                    c = lax.rem(my_stn + shift, stations)
                    source = out.at[par, c, u]
                    landing = landed.at[par, pl.ds(me * slots_each, slots_each)]
                    mine = jnp.logical_and(shift == 0, u == my_chan)

                    @pl.when(mine)
                    def _():
                        pltpu.make_async_copy(source, landing, recv_sem.at[par]).start()

                    @pl.when(jnp.logical_not(mine))
                    def _():
                        pltpu.make_async_remote_copy(
                            src_ref=source,
                            dst_ref=landing,
                            send_sem=send_sem.at[par],
                            recv_sem=recv_sem.at[par],
                            device_id=(c, u),
                            device_id_type=pl.DeviceIdType.MESH,
                        ).start()

        return blocks

    size = half // 2
    count = size // AVG
    own_half = my_chan // (spans // 2)
    for par in range(2):
        for turn in range(2):
            which = lax.rem(own_half + turn, 2)
            at = pl.multiple_of(which * size, size)
            table = tab_ref.at[par, pl.ds(pl.multiple_of(which * half, half), half)]

            @pl.loop(0, phases)
            def _(phase):
                transform(phase, at, g.at[par, phase], table, t1_ref.at[par], br, tw)

            bands(frames, br, out.at[par], which * count, lax.rem(my_chan // 2, count), emit(par))

    dims = (((1,), (1,)), ((), ()))
    height = rows_out.shape[2]

    def product(j, part):
        source = (x, y)[part]
        at = pl.multiple_of(j * height, height)
        return lax.dot_general(source[pl.ds(at, height), :], x[...], dims, preferred_element_type=jnp.float32)

    def arrived(par):
        pltpu.make_async_copy(landed.at[par], landed.at[par], recv_sem.at[par]).wait()

    arrived(0)
    spread(landed.at[0], wide, x, y)

    @pl.loop(0, stations)
    def _(j):
        for part in range(2):
            partial[j, part] = product(j, part)

    arrived(1)
    spread(landed.at[1], wide, x, y)

    def owner(turn):
        return lax.rem(my_stn + jnp.where(turn < 2, 2 + turn, 3 - turn), stations)

    def send(j, part):
        source, landing = rows_out.at[j, part], v_ref.at[my_stn, part]

        @pl.when(j == my_stn)
        def _():
            pltpu.make_async_copy(source, landing, row_recv).start()

        @pl.when(j != my_stn)
        def _():
            pltpu.make_async_remote_copy(
                src_ref=source,
                dst_ref=landing,
                send_sem=row_send,
                recv_sem=row_recv,
                device_id=(j, my_chan),
                device_id_type=pl.DeviceIdType.MESH,
            ).start()

    def finish(j, part):
        total = (partial[j, part] + product(j, part)) * scaling
        rows_out[j, part] = total.astype(rows_out.dtype)

    @pl.loop(0, stations)
    def _(turn):
        j = owner(turn)
        finish(j, 0)

        @pl.when(turn > 0)
        def _():
            send(owner(turn - 1), 1)

        finish(j, 1)
        send(j, 0)

    send(owner(stations - 1), 1)
    for i in range(inputs):
        others = inbox.at[i, pl.ds(0, lane_count - 1)]
        pltpu.make_async_copy(others, others, in_send.at[i]).wait()
    for par in range(2):
        others = landed.at[par, pl.ds(0, landed.shape[1] - slots_each)]
        pltpu.make_async_copy(others, others, send_sem.at[par]).wait()
    pltpu.make_async_copy(v_ref, v_ref, row_recv).wait()
    others = v_ref.at[pl.ds(0, stations - 1)]
    pltpu.make_async_copy(others, others, row_send).wait()


def correlate(voltages, fir_taps, spectra_count, scaling, stations, lane_count):
    rows_dev, fr, slots = voltages.shape
    phases = fir_taps.shape[0]
    inputs = rows_dev // lane_count
    frames = lane_count // phases * fr
    half = slots // 2
    rows = inputs * frames
    parts = rows // LANES
    spans = slots // AVG
    whole = pl.BlockSpec(memory_space=pltpu.VMEM)
    whole_inputs = stations * rows_dev
    depth = AVG // 2 * LANES
    table = np.stack([dft_table(slots, par) for par in range(2)])
    twist = jnp.stack([first_twist(slots, phases, par) for par in range(2)])
    return pl.pallas_call(
        lambda *refs: channelise_kernel(spectra_count, scaling, *refs),
        out_shape=jax.ShapeDtypeStruct((stations, 2, rows_dev, whole_inputs), jnp.bfloat16),
        in_specs=[pl.BlockSpec(memory_space=pl.ANY), whole, whole, whole],
        out_specs=pl.BlockSpec(memory_space=pl.ANY),
        scratch_shapes=[
            pltpu.VMEM((inputs, lane_count, fr, slots), jnp.bfloat16),
            pltpu.VMEM((slots // LANES, frames + 8, LANES), jnp.float32),
            pltpu.VMEM((2, phases, rows, slots), jnp.bfloat16),
            pltpu.VMEM((phases, 2, parts, half // 2, LANES), jnp.bfloat16),
            pltpu.VMEM((2, half // 2, LANES), jnp.float32),
            pltpu.VMEM((2, stations, spans, parts, AVG, LANES), jnp.bfloat16),
            pltpu.VMEM((2, stations * spans * parts, AVG, LANES), jnp.bfloat16),
            pltpu.VMEM((LANES * AVG // 2, LANES), jnp.float32),
            pltpu.VMEM((whole_inputs, depth), jnp.bfloat16),
            pltpu.VMEM((whole_inputs, depth), jnp.bfloat16),
            pltpu.VMEM((stations, 2, rows_dev, whole_inputs), jnp.float32),
            pltpu.VMEM((stations, 2, rows_dev, whole_inputs), jnp.bfloat16),
            pltpu.SemaphoreType.DMA((inputs,)),
            pltpu.SemaphoreType.DMA((inputs,)),
            pltpu.SemaphoreType.DMA((2,)),
            pltpu.SemaphoreType.DMA((2,)),
            pltpu.SemaphoreType.DMA,
            pltpu.SemaphoreType.DMA,
        ],
        compiler_params=pltpu.CompilerParams(vmem_limit_bytes=60 << 20, has_side_effects=True),
        cost_estimate=pl.CostEstimate(flops=30 * 10**9, bytes_accessed=20 << 20, transcendentals=0),
    )(voltages, fir_taps, jnp.asarray(table), twist)


def per_device(voltages, fir_taps):
    fr, slots = voltages.shape[2:]
    phases, taps, _ = fir_taps.shape
    lane_count = lax.axis_size("chan")
    stations = lax.axis_size("stn")
    spectra_count = lane_count // phases * fr - (taps - 1)
    scaling = 1.0 / (phases * slots * AVG * spectra_count)
    mine = correlate(voltages[:, 0], fir_taps, spectra_count, scaling, stations, lane_count)
    return mine.astype(jnp.float32)[:, None]


def solution(mesh):
    return jax.shard_map(
        per_device,
        mesh=mesh,
        in_specs=(P("stn", "chan", None, None), P()),
        out_specs=P(None, "chan", None, "stn", None),
        check_vma=False,
    )
```

time: 293 us -> 279 us (0.952)
  waiting for transfers between devices: 49.3 us -> 0 us
  Pallas kernels: 224 us -> 270 us
  starting transfers between devices: 9.85 us -> 0 us
    all_to_all x1 -> x0, waiting for transfers between devices: 49.3 us -> none  [per_device(): dealt = lax.all_to_all(voltages[:, 0], 'chan', 0, 0, tiled=True)]
    pallas_call x1, Pallas kernels: 224 us -> 270 us  [correlate(): pl.pallas_call(lambda *refs: channelise_kernel(spectra_count, scaling, *r...]
    all_to_all x1 -> x0, starting transfers between devices: 9.85 us -> none  [per_device(): dealt = lax.all_to_all(voltages[:, 0], 'chan', 0, 0, tiled=True)]
  transfers between devices with their start and end apart: 1 -> 0, of which waited for: 1 -> 0; matrix products, arithmetic and copies ran while one was open for 1% -> 0% of each run, Pallas kernels for 0% -> 0%
where the time goes in v4:
time: 279 us; the launch traced here: 278 us
  Pallas kernels  270 us (97%)
  other arithmetic  7.93 us (3%)
    pallas_call x1, Pallas kernels, correlate(): pl.pallas_call(lambda *refs: channelise_kernel(spectra_count, scaling, *r...  270 us
    broadcast_in_dim x1, other arithmetic, per_device(): return mine.astype(jnp.float32)[:, None]  6.64 us

profile of v4, /device:TPU:3, one launch (start us, length us, event | category | flops | bytes accessed | tf_op | source)
XLA Modules:
  0.0 278.5 jit_solution(11046632360731053095)
XLA Ops:
  0.2 0.1 broadcast_in_dim.23
  0.3 0.1 broadcast_in_dim.22
  0.5 0.1 broadcast_in_dim.25
  0.6 0.1 broadcast_in_dim.24
  0.7 0.1 maximum_bitcast_fusion
  0.8 1.0 pad_maximum_fusion.refs_3_
  1.8 270.0 %shard_map.37 = bf16[4,2,256,1024]{3,2,1,0:T(8,128)(2,1)} custom-call(bf16[256,8,1024]{2,1,0:T(8,128)(2,1)} %bitcast.11, f32[8,8,1024]{2,1,0:T(8,128)} %refs_1_.1, bf16[2,1024,1024]{2,1,0:T(8,128)(2,1)} %constant.8.clone.refs_2_, f32[2,2,512,128]{3,2,1,0:T(8,128)} %pad_maximum_fusion.refs_3_), custom_call_target="tpu_custom_call" | custom-call | flops 30000001024 | bytes 20971520 | tf_op jit(solution)/shard_map/pallas_call | solution.py:352
  271.9 6.6 %bitcast_convert_fusion = f32[4,1,2,256,1024]{4,3,2,1,0:T(8,128)} fusion(bf16[4,2,256,1024]{3,2,1,0:T(8,128)(2,1)} %shard_map.37), kind=kLoop, calls=%fused_computation | loop fusion | flops 2097152 | bytes 12582912 | tf_op jit(solution)/shard_map/broadcast_in_dim | solution.py:390
  (4 shorter events, 0.2 us)

commit v5 on v4

--- a/solution.py
+++ b/solution.py
@@ -289,27 +289,44 @@
     def owner(turn):
         return lax.rem(my_stn + jnp.where(turn < 2, 2 + turn, 3 - turn), stations)
 
+    def columns(j):
+        return pl.ds(pl.multiple_of(j * height, height), height)
+
     def send(j, part):
-        source, landing = rows_out.at[j, part], v_ref.at[my_stn, part]
+        def copies(fly):
+            lines = pl.ds(pl.multiple_of((2 * my_stn + part) * height, height), height)
+            if part == 0:
+                fly(rows_out.at[j, 0], v_ref.at[lines])
+            else:
+                for turn in range(1, stations):
+                    other = columns(lax.rem(j + turn, stations))
+                    fly(rows_out.at[j, 1, :, other], v_ref.at[lines, other])
 
         @pl.when(j == my_stn)
         def _():
-            pltpu.make_async_copy(source, landing, row_recv).start()
+            copies(lambda source, landing: pltpu.make_async_copy(source, landing, row_recv).start())
 
         @pl.when(j != my_stn)
         def _():
-            pltpu.make_async_remote_copy(
-                src_ref=source,
-                dst_ref=landing,
-                send_sem=row_send,
-                recv_sem=row_recv,
-                device_id=(j, my_chan),
-                device_id_type=pl.DeviceIdType.MESH,
-            ).start()
+            copies(
+                lambda source, landing: pltpu.make_async_remote_copy(
+                    src_ref=source,
+                    dst_ref=landing,
+                    send_sem=row_send,
+                    recv_sem=row_recv,
+                    device_id=(j, my_chan),
+                    device_id_type=pl.DeviceIdType.MESH,
+                ).start()
+            )
 
     def finish(j, part):
         total = (partial[j, part] + product(j, part)) * scaling
         rows_out[j, part] = total.astype(rows_out.dtype)
+        if part == 1:
+            row = lax.broadcasted_iota(jnp.int32, (height, height), 0)
+            col = lax.broadcasted_iota(jnp.int32, (height, height), 1)
+            both = [rows_out[j, p, :, columns(j)].astype(jnp.float32) for p in range(2)]
+            rows_out[j, 0, :, columns(j)] = jnp.where(row <= col, both[0], both[1]).astype(rows_out.dtype)
 
     @pl.loop(0, stations)
     def _(turn):
@@ -330,9 +347,35 @@
     for par in range(2):
         others = landed.at[par, pl.ds(0, landed.shape[1] - slots_each)]
         pltpu.make_async_copy(others, others, send_sem.at[par]).wait()
-    pltpu.make_async_copy(v_ref, v_ref, row_recv).wait()
-    others = v_ref.at[pl.ds(0, stations - 1)]
-    pltpu.make_async_copy(others, others, row_send).wait()
+    each = 2 * height - height // stations
+    for sem, count in ((row_recv, stations), (row_send, stations - 1)):
+        all_of = v_ref.at[pl.ds(0, count * each)]
+        pltpu.make_async_copy(all_of, all_of, sem).wait()
+
+
+def mirror_kernel(r_ref, o_ref):
+    height = r_ref.shape[0] // 2
+    j = lax.axis_index("stn")
+    at = pl.ds(pl.multiple_of(j * height, height), height)
+    for part in range(2):
+        o_ref[0, 0, part] = r_ref[part * height : (part + 1) * height].astype(jnp.float32)
+    row = lax.broadcasted_iota(jnp.int32, (height, height), 0)
+    col = lax.broadcasted_iota(jnp.int32, (height, height), 1)
+    both = r_ref[:height, at].astype(jnp.float32)
+    turned = both.T
+    o_ref[0, 0, 0, :, at] = jnp.where(row <= col, both, turned)
+    o_ref[0, 0, 1, :, at] = jnp.where(row > col, both, jnp.where(row < col, -turned, 0.0))
+
+
+def mirror(rows, stations):
+    height = rows.shape[0] // stations // 2
+    return pl.pallas_call(
+        mirror_kernel,
+        grid=(stations,),
+        out_shape=jax.ShapeDtypeStruct((stations, 1, 2, height, rows.shape[1]), jnp.float32),
+        in_specs=[pl.BlockSpec((2 * height, rows.shape[1]), lambda c: (c, 0))],
+        out_specs=pl.BlockSpec((1, 1, 2, height, rows.shape[1]), lambda c: (c, 0, 0, 0, 0)),
+    )(rows)
 
 
 def correlate(voltages, fir_taps, spectra_count, scaling, stations, lane_count):
@@ -351,7 +394,7 @@
     twist = jnp.stack([first_twist(slots, phases, par) for par in range(2)])
     return pl.pallas_call(
         lambda *refs: channelise_kernel(spectra_count, scaling, *refs),
-        out_shape=jax.ShapeDtypeStruct((stations, 2, rows_dev, whole_inputs), jnp.bfloat16),
+        out_shape=jax.ShapeDtypeStruct((stations * 2 * rows_dev, whole_inputs), jnp.bfloat16),
         in_specs=[pl.BlockSpec(memory_space=pl.ANY), whole, whole, whole],
         out_specs=pl.BlockSpec(memory_space=pl.ANY),
         scratch_shapes=[
@@ -387,7 +430,7 @@
     spectra_count = lane_count // phases * fr - (taps - 1)
     scaling = 1.0 / (phases * slots * AVG * spectra_count)
     mine = correlate(voltages[:, 0], fir_taps, spectra_count, scaling, stations, lane_count)
-    return mine.astype(jnp.float32)[:, None]
+    return mirror(mine, stations)
 
 
 def solution(mesh):

time: 279 us -> 267 us (0.957)
  other arithmetic: 7.93 us -> 1.29 us
  Pallas kernels: 270 us -> 265 us
    pallas_call x1, Pallas kernels: 270 us -> 259 us  [correlate(): pl.pallas_call(lambda *refs: channelise_kernel(spectra_count, scaling, *r...]
    broadcast_in_dim x1 -> x0, other arithmetic: 6.64 us -> none  [per_device(): return mine.astype(jnp.float32)[:, None]]
    pallas_call x0 -> x1, Pallas kernels: none -> 6.08 us  [mirror(): pl.pallas_call(mirror_kernel, grid=(stations,), out_shape=jax.ShapeDtypeS...]
where the time goes in v5:
time: 267 us
  Pallas kernels  265 us (99%)
    pallas_call x1, Pallas kernels, correlate(): pl.pallas_call(lambda *refs: channelise_kernel(spectra_count, scaling, *r...  259 us
    pallas_call x1, Pallas kernels, mirror(): pl.pallas_call(mirror_kernel, grid=(stations,), out_shape=jax.ShapeDtypeS...  6.08 us

profile of v5, /device:TPU:3, one launch (start us, length us, event | category | flops | bytes accessed | tf_op | source)
XLA Modules:
  0.0 266.8 jit_solution(8806179823828803998)
XLA Ops:
  0.2 0.1 broadcast_in_dim.17
  0.3 0.1 broadcast_in_dim.16
  0.5 0.1 broadcast_in_dim.19
  0.6 0.1 broadcast_in_dim.18
  0.7 0.1 maximum_bitcast_fusion
  0.8 1.0 pad_maximum_fusion.refs_3_
  1.8 258.8 %shard_map.37.r_ref = bf16[2048,1024]{1,0:T(8,128)(2,1)} custom-call(bf16[256,8,1024]{2,1,0:T(8,128)(2,1)} %bitcast.5, f32[8,8,1024]{2,1,0:T(8,128)} %refs_1_.1, bf16[2,1024,1024]{2,1,0:T(8,128)(2,1)} %constant.8.clone.refs_2_, f32[2,2,512,128]{3,2,1,0:T(8,128)} %pad_maximum_fusion.refs_3_), custom_call_target="tpu_custom_call" | custom-call | flops 30000001024 | bytes 20971520 | tf_op jit(solution)/shard_map/pallas_call | solution.py:395
  260.7 6.1 %shard_map.38 = f32[4,1,2,256,1024]{4,3,2,1,0:T(8,128)} custom-call(bf16[2048,1024]{1,0:T(8,128)(2,1)} %shard_map.37.r_ref), custom_call_target="tpu_custom_call" | custom-call | tf_op jit(solution)/shard_map/pallas_call | solution.py:372
  (4 shorter events, 0.2 us)

commit v6 on v5

--- a/solution.py
+++ b/solution.py
@@ -26,10 +26,9 @@
 
 def first_twist(slots, phases, par):
     half = slots // 2
-    q = 2 * jnp.arange(half, dtype=jnp.int32) + par
-    q = jnp.broadcast_to(q[:, None], (half, LANES))
-    angles = q.astype(jnp.float32) * jnp.float32(-2.0 * math.pi / (phases * slots))
-    return jnp.stack([jnp.cos(angles), jnp.sin(angles)])
+    q = 2 * np.arange(half, dtype=np.float64) + par
+    angles = np.broadcast_to(q[:, None], (half, LANES)) * (-2.0 * math.pi / (phases * slots))
+    return np.stack([np.cos(angles), np.sin(angles)]).astype(np.float32)
 
 
 def transform(phase, at, g, tab_ref, t1_ref, br, tw):
@@ -391,7 +390,7 @@
     whole_inputs = stations * rows_dev
     depth = AVG // 2 * LANES
     table = np.stack([dft_table(slots, par) for par in range(2)])
-    twist = jnp.stack([first_twist(slots, phases, par) for par in range(2)])
+    twist = np.stack([first_twist(slots, phases, par) for par in range(2)])
     return pl.pallas_call(
         lambda *refs: channelise_kernel(spectra_count, scaling, *refs),
         out_shape=jax.ShapeDtypeStruct((stations * 2 * rows_dev, whole_inputs), jnp.bfloat16),
@@ -419,7 +418,7 @@
         ],
         compiler_params=pltpu.CompilerParams(vmem_limit_bytes=60 << 20, has_side_effects=True),
         cost_estimate=pl.CostEstimate(flops=30 * 10**9, bytes_accessed=20 << 20, transcendentals=0),
-    )(voltages, fir_taps, jnp.asarray(table), twist)
+    )(voltages, fir_taps, jnp.asarray(table), jnp.asarray(twist))
 
 
 def per_device(voltages, fir_taps):

time: 267 us -> 265 us (level)
  no operation moved by 1% of the time
where the time goes in v6:
time: 265 us
  Pallas kernels  265 us (100%)
    pallas_call x1, Pallas kernels, correlate(): pl.pallas_call(lambda *refs: channelise_kernel(spectra_count, scaling, *r...  259 us
    pallas_call x1, Pallas kernels, mirror(): pl.pallas_call(mirror_kernel, grid=(stations,), out_shape=jax.ShapeDtypeS...  6.08 us

profile of v6, /device:TPU:3, one launch (start us, length us, event | category | flops | bytes accessed | tf_op | source)
XLA Modules:
  0.0 264.9 jit_solution(8575029820408876229)
XLA Ops:
  0.0 258.8 %shard_map.46.r_ref = bf16[2048,1024]{1,0:T(8,128)(2,1)} custom-call(bf16[256,8,1024]{2,1,0:T(8,128)(2,1)} %bitcast.1, f32[8,8,1024]{2,1,0:T(8,128)} %refs_1_.1, bf16[2,1024,1024]{2,1,0:T(8,128)(2,1)} %constant.4.clone.refs_2_, f32[2,2,512,128]{3,2,1,0:T(8,128)} %constant.5.clone.refs_3_), custom_call_target="tpu_custom_call" | custom-call | flops 30000001024 | bytes 20971520 | tf_op jit(solution)/shard_map/pallas_call | solution.py:394
  258.8 6.1 %shard_map.47 = f32[4,1,2,256,1024]{4,3,2,1,0:T(8,128)} custom-call(bf16[2048,1024]{1,0:T(8,128)(2,1)} %shard_map.46.r_ref), custom_call_target="tpu_custom_call" | custom-call | tf_op jit(solution)/shard_map/pallas_call | solution.py:371
